TPU v7x, 32 devices: a 4x4x1 block of a 4x4x8 slice. The times are simulated.
32 devices in a mesh: batch: 1 (over z), col: 4 (over y), row: 8 (over x, core).
Axes of the slice: x: 4, y: 4, z: 1, core: 2. Of those that a mesh axis runs over, the one named last changes fastest.
The devices are a block of a 4x4x8 slice.
Arguments:
- images: bfloat16 [16, 256, 512, 64], P('batch', 'row', 'col')
- w_down1: bfloat16 [4, 4, 64, 128], replicated
- b_down1: float32 [128], replicated
- w_conv1: bfloat16 [3, 3, 128, 128], replicated
- b_conv1: float32 [128], replicated
- w_down2: bfloat16 [4, 4, 128, 256], replicated
- b_down2: float32 [256], replicated
- w_conv2: bfloat16 [3, 3, 256, 256], replicated
- b_conv2: float32 [256], replicated
- w_down3: bfloat16 [4, 4, 256, 320], replicated
- b_down3: float32 [320], replicated
- w_conv3: bfloat16 [3, 3, 320, 320], replicated
- b_conv3: float32 [320], replicated
Outputs:
- output: bfloat16 [16, 32, 64, 320], P('batch', 'row', 'col')
All inputs are finite; a program needn't handle non-finite values.
Results may differ from a plain program's by a relative error of at most 0.00703317.
Values are sent between devices in bfloat16 or wider.
A program may use at most 768 MiB of HBM per device.

v0:
```python
import jax
import jax.numpy as jnp
from jax import lax
from jax.sharding import PartitionSpec as P


def solution(mesh):
    row_len = mesh.shape['row']
    col_len = mesh.shape['col']

    def add_halo(act_tile, axis_name, edge_dim, axis_len):
        if edge_dim == 1:
            head_edge = act_tile[:, :1]
            tail_edge = act_tile[:, -1:]
        else:
            head_edge = act_tile[:, :, :1]
            tail_edge = act_tile[:, :, -1:]
        if axis_len == 1:
            from_prev = jnp.zeros_like(tail_edge)
            from_next = jnp.zeros_like(head_edge)
        else:
            to_next = [(i, i + 1) for i in range(axis_len - 1)]
            to_prev = [(i + 1, i) for i in range(axis_len - 1)]
            from_prev = lax.ppermute(tail_edge, axis_name, to_next)
            from_next = lax.ppermute(head_edge, axis_name, to_prev)
        return jnp.concatenate([from_prev, act_tile, from_next], axis=edge_dim)

    def conv_relu(act_tile, weight, bias_vec, stride):
        padded = add_halo(add_halo(act_tile, 'row', 1, row_len), 'col', 2, col_len)
        summed = lax.conv_general_dilated(padded, weight, (stride, stride), 'VALID', dimension_numbers=('NHWC', 'HWIO', 'NHWC'), preferred_element_type=jnp.float32)
        return jax.nn.relu(summed + bias_vec).astype(jnp.bfloat16)

    def local_encoder(images, w_down1, b_down1, w_conv1, b_conv1, w_down2, b_down2, w_conv2, b_conv2, w_down3, b_down3, w_conv3, b_conv3):
        params = [(w_down1, b_down1, w_conv1, b_conv1), (w_down2, b_down2, w_conv2, b_conv2), (w_down3, b_down3, w_conv3, b_conv3)]
        act_tile = images
        for w_down, b_down, w_conv, b_conv in params:
            act_tile = conv_relu(act_tile, w_down, b_down, 2)
            act_tile = conv_relu(act_tile, w_conv, b_conv, 1)
        return act_tile

    tile_spec = P('batch', 'row', 'col', None)
    return jax.shard_map(local_encoder, mesh=mesh, in_specs=(tile_spec,) + (P(),) * 12, out_specs=tile_spec, check_vma=False)
```

profile of v0, /device:TPU:97, one launch (start us, length us, event | category | flops | bytes accessed | tf_op | source)
XLA Modules:
  0.0 187.3 jit_solution(16501399976888667410)
XLA Ops:
  0.0 18.9 %copy.14 = bf16[16,32,128,64]{3,0,2,1:T(8,128)(2,1)} copy(bf16[16,32,128,64]{2,3,1,0:T(8,128)(2,1)} %param.13) | data formatting | bytes 16777216 | tf_op args[0]
  18.9 1.4 fusion.75
  20.3 4.6 %collective-permute-start = (bf16[16,1,128,64]{3,0,2,1:T(8,128)(2,1)S(1)}, bf16[16,1,128,64]{3,0,2,1:T(8,128)(2,1)S(1)}, u32[]{:S(2)}, u32[]{:S(2)}) collective-permute-start(bf16[16,1,128,64]{3,0,2,1:T(8,128)(2,1)S(1)} %get-tuple-element.7), channel_id=1, source_target_pairs={{0,1},{1,2},{2,3},{3,4},{4,5},{5,6},{6,7},{8,9},{9,10},{10,11},{11... | collective-permute-start | bytes 786440 | tf_op jit(solution)/shard_map/ppermute | solution.py:24
  24.9 2.3 %collective-permute-start.1 = (bf16[16,1,128,64]{3,0,2,1:T(8,128)(2,1)S(1)}, bf16[16,1,128,64]{3,0,2,1:T(8,128)(2,1)S(1)}, u32[]{:S(2)}, u32[]{:S(2)}) collective-permute-start(bf16[16,1,128,64]{3,0,2,1:T(8,128)(2,1)S(1)} %get-tuple-element.8), channel_id=1, source_target_pairs={{1,0},{2,1},{3,2},{4,3},{5,4},{6,5},{7,6},{9,8},{10,9},{11,10},{12... | collective-permute-start | bytes 786440 | tf_op jit(solution)/shard_map/ppermute | solution.py:25
  27.3 3.7 %collective-permute-done = bf16[16,1,128,64]{3,0,2,1:T(8,128)(2,1)S(1)} collective-permute-done((bf16[16,1,128,64]{3,0,2,1:T(8,128)(2,1)S(1)}, bf16[16,1,128,64]{3,0,2,1:T(8,128)(2,1)S(1)}, u32[]{:S(2)}, u32[]{:S(2)}) %collective-permute-start) | collective-permute-done | bytes 262176 | tf_op jit(solution)/shard_map/ppermute | solution.py:24
  31.0 4.9 %collective-permute-done.1 = bf16[16,1,128,64]{3,0,2,1:T(8,128)(2,1)S(1)} collective-permute-done((bf16[16,1,128,64]{3,0,2,1:T(8,128)(2,1)S(1)}, bf16[16,1,128,64]{3,0,2,1:T(8,128)(2,1)S(1)}, u32[]{:S(2)}, u32[]{:S(2)}) %collective-permute-start.1) | collective-permute-done | bytes 262176 | tf_op jit(solution)/shard_map/ppermute | solution.py:25
  36.9 4.1 %collective-permute-start.2 = (bf16[16,34,1,64]{3,0,2,1:T(8,128)(2,1)S(1)}, bf16[16,34,1,64]{3,0,2,1:T(8,128)(2,1)S(1)}, u32[]{:S(2)}, u32[]{:S(2)}) collective-permute-start(bf16[16,34,1,64]{3,0,2,1:T(8,128)(2,1)S(1)} %get-tuple-element.5), channel_id=1, source_target_pairs={{0,8},{8,16},{16,24},{1,9},{9,17},{17,25},{2,10},{10,18},{18,26},{... | collective-permute-start | bytes 208904 | tf_op jit(solution)/shard_map/ppermute | solution.py:24
  41.0 1.3 collective-permute-start.3
  43.0 4.2 %collective-permute-done.3 = bf16[16,34,1,64]{3,0,2,1:T(8,128)(2,1)S(1)} collective-permute-done((bf16[16,34,1,64]{3,0,2,1:T(8,128)(2,1)S(1)}, bf16[16,34,1,64]{3,0,2,1:T(8,128)(2,1)S(1)}, u32[]{:S(2)}, u32[]{:S(2)}) %collective-permute-start.3) | collective-permute-done | bytes 69664 | tf_op jit(solution)/shard_map/ppermute | solution.py:25
  47.2 17.5 %maximum_convert_fusion.1 = bf16[16,16,64,128]{3,0,2,1:T(8,128)(2,1)S(1)} fusion(f32[128]{0:T(128)S(1)} %copy-done.11, bf16[4,4,64,128]{3,2,1,0:T(8,128)(2,1)S(1)} %copy-done.6, bf16[16,34,1,64]{3,0,2,1:T(8,128)(2,1)S(1)} %collective-permute-done.3, bf16[16,1,128,64]{3,0,2,1:T(8,128)(2,1)S(1)} %collective-permute-done.1, ...), kind=kOutput, calls=%fused_computation.11 | convolution fusion | flops 4319363072 | bytes 13509120 | tf_op jit(solution)/shard_map/conv_general_dilated | solution.py:30
  64.8 3.3 %collective-permute-start.4 = (bf16[16,1,64,128]{3,0,2,1:T(8,128)(2,1)S(1)}, bf16[16,1,64,128]{3,0,2,1:T(8,128)(2,1)S(1)}, u32[]{:S(2)}, u32[]{:S(2)}) collective-permute-start(bf16[16,1,64,128]{3,0,2,1:T(8,128)(2,1)S(1)} %get-tuple-element.15), channel_id=1, source_target_pairs={{0,1},{1,2},{2,3},{3,4},{4,5},{5,6},{6,7},{8,9},{9,10},{10,11},{11... | collective-permute-start | bytes 786440 | tf_op jit(solution)/shard_map/ppermute | solution.py:24
  68.1 2.0 %collective-permute-start.5 = (bf16[16,1,64,128]{3,0,2,1:T(8,128)(2,1)S(1)}, bf16[16,1,64,128]{3,0,2,1:T(8,128)(2,1)S(1)}, u32[]{:S(2)}, u32[]{:S(2)}) collective-permute-start(bf16[16,1,64,128]{3,0,2,1:T(8,128)(2,1)S(1)} %get-tuple-element.16), channel_id=1, source_target_pairs={{1,0},{2,1},{3,2},{4,3},{5,4},{6,5},{7,6},{9,8},{10,9},{11,10},{12... | collective-permute-start | bytes 786440 | tf_op jit(solution)/shard_map/ppermute | solution.py:25
  70.0 1.3 collective-permute-done.4
  71.3 4.4 %collective-permute-done.5 = bf16[16,1,64,128]{3,0,2,1:T(8,128)(2,1)S(1)} collective-permute-done((bf16[16,1,64,128]{3,0,2,1:T(8,128)(2,1)S(1)}, bf16[16,1,64,128]{3,0,2,1:T(8,128)(2,1)S(1)}, u32[]{:S(2)}, u32[]{:S(2)}) %collective-permute-start.5) | collective-permute-done | bytes 262176 | tf_op jit(solution)/shard_map/ppermute | solution.py:25
  75.8 3.9 %collective-permute-start.6 = (bf16[16,18,1,128]{3,0,2,1:T(8,128)(2,1)S(1)}, bf16[16,18,1,128]{3,0,2,1:T(8,128)(2,1)S(1)}, u32[]{:S(2)}, u32[]{:S(2)}) collective-permute-start(bf16[16,18,1,128]{3,0,2,1:T(8,128)(2,1)S(1)} %get-tuple-element.11), channel_id=1, source_target_pairs={{0,8},{8,16},{16,24},{1,9},{9,17},{17,25},{2,10},{10,18},{18,26},{... | collective-permute-start | bytes 221192 | tf_op jit(solution)/shard_map/ppermute | solution.py:24
  79.7 1.5 collective-permute-start.7
  81.2 3.8 %collective-permute-done.7 = bf16[16,18,1,128]{3,0,2,1:T(8,128)(2,1)S(1)} collective-permute-done((bf16[16,18,1,128]{3,0,2,1:T(8,128)(2,1)S(1)}, bf16[16,18,1,128]{3,0,2,1:T(8,128)(2,1)S(1)}, u32[]{:S(2)}, u32[]{:S(2)}) %collective-permute-start.7) | collective-permute-done | bytes 73760 | tf_op jit(solution)/shard_map/ppermute | solution.py:25
  85.0 10.3 %maximum_convert_fusion = bf16[16,16,64,128]{3,0,2,1:T(8,128)(2,1)S(1)} fusion(f32[128]{0:T(128)S(1)} %copy-done.12, bf16[3,3,128,128]{3,2,1,0:T(8,128)(2,1)S(1)} %copy-done.5, bf16[16,18,1,128]{3,0,2,1:T(8,128)(2,1)S(1)} %collective-permute-done.7, bf16[16,1,64,128]{3,0,2,1:T(8,128)(2,1)S(1)} %collective-permute-done.5, ...), kind=kOutput, calls=%fused_computation.10 | convolution fusion | flops 4847861760 | bytes 9355776 | tf_op jit(solution)/shard_map/conv_general_dilated | solution.py:30
  95.3 3.1 %collective-permute-start.8 = (bf16[16,1,64,128]{3,0,2,1:T(8,128)(2,1)S(1)}, bf16[16,1,64,128]{3,0,2,1:T(8,128)(2,1)S(1)}, u32[]{:S(2)}, u32[]{:S(2)}) collective-permute-start(bf16[16,1,64,128]{3,0,2,1:T(8,128)(2,1)S(1)} %get-tuple-element.13), channel_id=1, source_target_pairs={{0,1},{1,2},{2,3},{3,4},{4,5},{5,6},{6,7},{8,9},{9,10},{10,11},{11... | collective-permute-start | bytes 786440 | tf_op jit(solution)/shard_map/ppermute | solution.py:24
  98.5 2.0 %collective-permute-start.9 = (bf16[16,1,64,128]{3,0,2,1:T(8,128)(2,1)S(1)}, bf16[16,1,64,128]{3,0,2,1:T(8,128)(2,1)S(1)}, u32[]{:S(2)}, u32[]{:S(2)}) collective-permute-start(bf16[16,1,64,128]{3,0,2,1:T(8,128)(2,1)S(1)} %get-tuple-element.14), channel_id=1, source_target_pairs={{1,0},{2,1},{3,2},{4,3},{5,4},{6,5},{7,6},{9,8},{10,9},{11,10},{12... | collective-permute-start | bytes 786440 | tf_op jit(solution)/shard_map/ppermute | solution.py:25
  100.4 1.3 collective-permute-done.8
  101.8 4.4 %collective-permute-done.9 = bf16[16,1,64,128]{3,0,2,1:T(8,128)(2,1)S(1)} collective-permute-done((bf16[16,1,64,128]{3,0,2,1:T(8,128)(2,1)S(1)}, bf16[16,1,64,128]{3,0,2,1:T(8,128)(2,1)S(1)}, u32[]{:S(2)}, u32[]{:S(2)}) %collective-permute-start.9) | collective-permute-done | bytes 262176 | tf_op jit(solution)/shard_map/ppermute | solution.py:25
  106.2 3.6 %collective-permute-start.10 = (bf16[16,18,1,128]{3,0,2,1:T(8,128)(2,1)S(1)}, bf16[16,18,1,128]{3,0,2,1:T(8,128)(2,1)S(1)}, u32[]{:S(2)}, u32[]{:S(2)}) collective-permute-start(bf16[16,18,1,128]{3,0,2,1:T(8,128)(2,1)S(1)} %get-tuple-element.9), channel_id=1, source_target_pairs={{0,8},{8,16},{16,24},{1,9},{9,17},{17,25},{2,10},{10,18},{18,26},{... | collective-permute-start | bytes 221192 | tf_op jit(solution)/shard_map/ppermute | solution.py:24
  109.8 1.4 collective-permute-start.11
  111.3 3.8 %collective-permute-done.11 = bf16[16,18,1,128]{3,0,2,1:T(8,128)(2,1)S(1)} collective-permute-done((bf16[16,18,1,128]{3,0,2,1:T(8,128)(2,1)S(1)}, bf16[16,18,1,128]{3,0,2,1:T(8,128)(2,1)S(1)}, u32[]{:S(2)}, u32[]{:S(2)}) %collective-permute-start.11) | collective-permute-done | bytes 73760 | tf_op jit(solution)/shard_map/ppermute | solution.py:25
  115.1 4.8 %maximum_convert_fusion.3 = bf16[16,8,32,256]{3,0,2,1:T(8,128)(2,1)S(1)} fusion(f32[256]{0:T(256)S(1)} %copy-done.9, bf16[4,4,128,256]{3,2,1,0:T(8,128)(2,1)S(1)} %copy-done.4, bf16[16,18,1,128]{3,0,2,1:T(8,128)(2,1)S(1)} %collective-permute-done.11, bf16[16,1,64,128]{3,0,2,1:T(8,128)(2,1)S(1)} %collective-permute-done.9, ...), kind=kOutput, calls=%fused_computation.33 | convolution fusion | flops 4307845120 | bytes 8012800 | tf_op jit(solution)/shard_map/conv_general_dilated | solution.py:30
  119.9 3.2 %collective-permute-start.12 = (bf16[16,1,32,256]{3,0,2,1:T(8,128)(2,1)S(1)}, bf16[16,1,32,256]{3,0,2,1:T(8,128)(2,1)S(1)}, u32[]{:S(2)}, u32[]{:S(2)}) collective-permute-start(bf16[16,1,32,256]{3,0,2,1:T(8,128)(2,1)S(1)} %get-tuple-element.23), channel_id=1, source_target_pairs={{0,1},{1,2},{2,3},{3,4},{4,5},{5,6},{6,7},{8,9},{9,10},{10,11},{11... | collective-permute-start | bytes 786440 | tf_op jit(solution)/shard_map/ppermute | solution.py:24
  123.1 2.0 %collective-permute-start.13 = (bf16[16,1,32,256]{3,0,2,1:T(8,128)(2,1)S(1)}, bf16[16,1,32,256]{3,0,2,1:T(8,128)(2,1)S(1)}, u32[]{:S(2)}, u32[]{:S(2)}) collective-permute-start(bf16[16,1,32,256]{3,0,2,1:T(8,128)(2,1)S(1)} %get-tuple-element.24), channel_id=1, source_target_pairs={{1,0},{2,1},{3,2},{4,3},{5,4},{6,5},{7,6},{9,8},{10,9},{11,10},{12... | collective-permute-start | bytes 786440 | tf_op jit(solution)/shard_map/ppermute | solution.py:25
  125.1 1.3 collective-permute-done.12
  126.4 4.4 %collective-permute-done.13 = bf16[16,1,32,256]{3,0,2,1:T(8,128)(2,1)S(1)} collective-permute-done((bf16[16,1,32,256]{3,0,2,1:T(8,128)(2,1)S(1)}, bf16[16,1,32,256]{3,0,2,1:T(8,128)(2,1)S(1)}, u32[]{:S(2)}, u32[]{:S(2)}) %collective-permute-start.13) | collective-permute-done | bytes 262176 | tf_op jit(solution)/shard_map/ppermute | solution.py:25
  130.9 1.7 collective-permute-start.14
  134.0 3.8 %collective-permute-done.15 = bf16[16,10,1,256]{3,0,2,1:T(8,128)(2,1)S(1)} collective-permute-done((bf16[16,10,1,256]{3,0,2,1:T(8,128)(2,1)S(1)}, bf16[16,10,1,256]{3,0,2,1:T(8,128)(2,1)S(1)}, u32[]{:S(2)}, u32[]{:S(2)}) %collective-permute-start.15) | collective-permute-done | bytes 81952 | tf_op jit(solution)/shard_map/ppermute | solution.py:25
  137.8 5.3 %maximum_convert_fusion.2 = bf16[16,8,32,256]{3,0,2,1:T(8,128)(2,1)S(1)} fusion(f32[256]{0:T(256)S(1)} %copy-done.10, bf16[3,3,256,256]{3,2,1,0:T(8,128)(2,1)S(1)} %copy-done.3, bf16[16,10,1,256]{3,0,2,1:T(8,128)(2,1)S(1)} %collective-permute-done.15, bf16[16,1,32,256]{3,0,2,1:T(8,128)(2,1)S(1)} %collective-permute-done.13, ...), kind=kOutput, calls=%fused_computation.32 | convolution fusion | flops 4840554496 | bytes 6063104 | tf_op jit(solution)/shard_map/conv_general_dilated | solution.py:30
  143.2 3.2 %collective-permute-start.16 = (bf16[16,1,32,256]{3,0,2,1:T(8,128)(2,1)S(1)}, bf16[16,1,32,256]{3,0,2,1:T(8,128)(2,1)S(1)}, u32[]{:S(2)}, u32[]{:S(2)}) collective-permute-start(bf16[16,1,32,256]{3,0,2,1:T(8,128)(2,1)S(1)} %get-tuple-element.21), channel_id=1, source_target_pairs={{0,1},{1,2},{2,3},{3,4},{4,5},{5,6},{6,7},{8,9},{9,10},{10,11},{11... | collective-permute-start | bytes 786440 | tf_op jit(solution)/shard_map/ppermute | solution.py:24
  146.4 2.0 %collective-permute-start.17 = (bf16[16,1,32,256]{3,0,2,1:T(8,128)(2,1)S(1)}, bf16[16,1,32,256]{3,0,2,1:T(8,128)(2,1)S(1)}, u32[]{:S(2)}, u32[]{:S(2)}) collective-permute-start(bf16[16,1,32,256]{3,0,2,1:T(8,128)(2,1)S(1)} %get-tuple-element.22), channel_id=1, source_target_pairs={{1,0},{2,1},{3,2},{4,3},{5,4},{6,5},{7,6},{9,8},{10,9},{11,10},{12... | collective-permute-start | bytes 786440 | tf_op jit(solution)/shard_map/ppermute | solution.py:25
  148.4 1.3 collective-permute-done.16
  149.7 4.4 %collective-permute-done.17 = bf16[16,1,32,256]{3,0,2,1:T(8,128)(2,1)S(1)} collective-permute-done((bf16[16,1,32,256]{3,0,2,1:T(8,128)(2,1)S(1)}, bf16[16,1,32,256]{3,0,2,1:T(8,128)(2,1)S(1)}, u32[]{:S(2)}, u32[]{:S(2)}) %collective-permute-start.17) | collective-permute-done | bytes 262176 | tf_op jit(solution)/shard_map/ppermute | solution.py:25
  154.1 1.7 collective-permute-start.18
  155.9 1.7 collective-permute-start.19
  157.5 3.7 %collective-permute-done.19 = bf16[16,10,1,256]{3,0,2,1:T(8,128)(2,1)S(1)} collective-permute-done((bf16[16,10,1,256]{3,0,2,1:T(8,128)(2,1)S(1)}, bf16[16,10,1,256]{3,0,2,1:T(8,128)(2,1)S(1)}, u32[]{:S(2)}, u32[]{:S(2)}) %collective-permute-start.19) | collective-permute-done | bytes 81952 | tf_op jit(solution)/shard_map/ppermute | solution.py:25
  161.2 4.6 %maximum_convert_fusion.5 = bf16[16,4,16,320]{3,0,2,1:T(8,128)(2,1)S(1)} fusion(bf16[4,4,256,320]{2,3,1,0:T(8,128)(2,1)S(1)} %copy-done, bf16[16,10,1,256]{3,0,2,1:T(8,128)(2,1)S(1)} %collective-permute-done.19, bf16[16,1,32,256]{3,0,2,1:T(8,128)(2,1)S(1)} %collective-permute-done.17, bf16[16,8,32,256]{3,0,2,1:T(8,128)(2,1)S(1)} %maximum_convert_fusion.2, ...), kind=kOutput, calls=%fused_computation.55 | convolution fusion | flops 2690908160 | bytes 6063360 | tf_op jit(solution)/shard_map/conv_general_dilated | solution.py:30
  165.8 3.2 %collective-permute-start.20 = (bf16[16,1,16,320]{3,0,2,1:T(8,128)(2,1)S(1)}, bf16[16,1,16,320]{3,0,2,1:T(8,128)(2,1)S(1)}, u32[]{:S(2)}, u32[]{:S(2)}) collective-permute-start(bf16[16,1,16,320]{3,0,2,1:T(8,128)(2,1)S(1)} %get-tuple-element.27), channel_id=1, source_target_pairs={{0,1},{1,2},{2,3},{3,4},{4,5},{5,6},{6,7},{8,9},{9,10},{10,11},{11... | collective-permute-start | bytes 491528 | tf_op jit(solution)/shard_map/ppermute | solution.py:24
  169.0 2.0 %collective-permute-start.21 = (bf16[16,1,16,320]{3,0,2,1:T(8,128)(2,1)S(1)}, bf16[16,1,16,320]{3,0,2,1:T(8,128)(2,1)S(1)}, u32[]{:S(2)}, u32[]{:S(2)}) collective-permute-start(bf16[16,1,16,320]{3,0,2,1:T(8,128)(2,1)S(1)} %get-tuple-element.28), channel_id=1, source_target_pairs={{1,0},{2,1},{3,2},{4,3},{5,4},{6,5},{7,6},{9,8},{10,9},{11,10},{12... | collective-permute-start | bytes 491528 | tf_op jit(solution)/shard_map/ppermute | solution.py:25
  171.6 4.4 %collective-permute-done.21 = bf16[16,1,16,320]{3,0,2,1:T(8,128)(2,1)S(1)} collective-permute-done((bf16[16,1,16,320]{3,0,2,1:T(8,128)(2,1)S(1)}, bf16[16,1,16,320]{3,0,2,1:T(8,128)(2,1)S(1)}, u32[]{:S(2)}, u32[]{:S(2)}) %collective-permute-start.21) | collective-permute-done | bytes 163872 | tf_op jit(solution)/shard_map/ppermute | solution.py:25
  176.1 1.7 collective-permute-start.22
  177.8 1.3 collective-permute-start.23
  179.1 3.7 %collective-permute-done.23 = bf16[16,6,1,320]{3,0,2,1:T(8,128)(2,1)S(1)} collective-permute-done((bf16[16,6,1,320]{3,0,2,1:T(8,128)(2,1)S(1)}, bf16[16,6,1,320]{3,0,2,1:T(8,128)(2,1)S(1)}, u32[]{:S(2)}, u32[]{:S(2)}) %collective-permute-start.23) | collective-permute-done | bytes 61472 | tf_op jit(solution)/shard_map/ppermute | solution.py:25
  182.9 3.4 %maximum_convert_fusion.4 = bf16[16,4,16,320]{3,0,2,1:T(8,128)(2,1)S(1)} fusion(bf16[3,3,320,320]{3,2,1,0:T(8,128)(2,1)S(1)} %copy-done.2, bf16[16,6,1,320]{3,0,2,1:T(8,128)(2,1)S(1)} %collective-permute-done.23, bf16[16,1,16,320]{3,0,2,1:T(8,128)(2,1)S(1)} %collective-permute-done.21, bf16[16,4,16,320]{3,0,2,1:T(8,128)(2,1)S(1)} %maximum_convert_fusion.5, ...), kind=kOutput, calls=%fused_computation.54 | convolution fusion | flops 1890631680 | bytes 3605760 | tf_op jit(solution)/shard_map/conv_general_dilated | solution.py:30
  (46 shorter events, 5.3 us)
Async XLA Ops:
  0.0 161.2 %copy-start = (bf16[4,4,256,320]{2,3,1,0:T(8,128)(2,1)S(1)}, bf16[4,4,256,320]{2,3,1,0:T(8,128)(2,1)}, u32[]{:S(2)}) copy-start(bf16[4,4,256,320]{2,3,1,0:T(8,128)(2,1)} %param.22) | copy-start | bytes 7864324
  20.3 10.7 %collective-permute-start = (bf16[16,1,128,64]{3,0,2,1:T(8,128)(2,1)S(1)}, bf16[16,1,128,64]{3,0,2,1:T(8,128)(2,1)S(1)}, u32[]{:S(2)}, u32[]{:S(2)}) collective-permute-start(bf16[16,1,128,64]{3,0,2,1:T(8,128)(2,1)S(1)} %get-tuple-element.7), channel_id=1, source_target_pairs={{0,1},{1,2},{2,3},{3,4},{4,5},{5,6},{6,7},{8,9},{9,10},{10,11},{11... | collective-permute-start | bytes 786440 | tf_op jit(solution)/shard_map/ppermute | solution.py:24
  24.9 22.3 %copy-start.1 = (bf16[16,32,128,64]{3,0,2,1:T(8,128)(2,1)S(1)}, bf16[16,32,128,64]{3,0,2,1:T(8,128)(2,1)}, u32[]{:S(2)}) copy-start(bf16[16,32,128,64]{3,0,2,1:T(8,128)(2,1)} %copy.14) | copy-start | bytes 25165828
  24.9 22.3 %copy-start.6 = (bf16[4,4,64,128]{3,2,1,0:T(8,128)(2,1)S(1)}, bf16[4,4,64,128]{3,2,1,0:T(8,128)(2,1)}, u32[]{:S(2)}) copy-start(bf16[4,4,64,128]{3,2,1,0:T(8,128)(2,1)} %param.14) | copy-start | bytes 786436
  24.9 22.3 %copy-start.11 = (f32[128]{0:T(128)S(1)}, f32[128]{0:T(128)}, u32[]{:S(2)}) copy-start(f32[128]{0:T(128)} %param.15) | copy-start | bytes 1540
  24.9 10.9 %collective-permute-start.1 = (bf16[16,1,128,64]{3,0,2,1:T(8,128)(2,1)S(1)}, bf16[16,1,128,64]{3,0,2,1:T(8,128)(2,1)S(1)}, u32[]{:S(2)}, u32[]{:S(2)}) collective-permute-start(bf16[16,1,128,64]{3,0,2,1:T(8,128)(2,1)S(1)} %get-tuple-element.8), channel_id=1, source_target_pairs={{1,0},{2,1},{3,2},{4,3},{5,4},{6,5},{7,6},{9,8},{10,9},{11,10},{12... | collective-permute-start | bytes 786440 | tf_op jit(solution)/shard_map/ppermute | solution.py:25
  36.9 6.1 %collective-permute-start.2 = (bf16[16,34,1,64]{3,0,2,1:T(8,128)(2,1)S(1)}, bf16[16,34,1,64]{3,0,2,1:T(8,128)(2,1)S(1)}, u32[]{:S(2)}, u32[]{:S(2)}) collective-permute-start(bf16[16,34,1,64]{3,0,2,1:T(8,128)(2,1)S(1)} %get-tuple-element.5), channel_id=1, source_target_pairs={{0,8},{8,16},{16,24},{1,9},{9,17},{17,25},{2,10},{10,18},{18,26},{... | collective-permute-start | bytes 208904 | tf_op jit(solution)/shard_map/ppermute | solution.py:24
  41.0 6.2 %collective-permute-start.3 = (bf16[16,34,1,64]{3,0,2,1:T(8,128)(2,1)S(1)}, bf16[16,34,1,64]{3,0,2,1:T(8,128)(2,1)S(1)}, u32[]{:S(2)}, u32[]{:S(2)}) collective-permute-start(bf16[16,34,1,64]{3,0,2,1:T(8,128)(2,1)S(1)} %get-tuple-element.6), channel_id=1, source_target_pairs={{8,0},{16,8},{24,16},{9,1},{17,9},{25,17},{10,2},{18,10},{26,18},{... | collective-permute-start | bytes 208904 | tf_op jit(solution)/shard_map/ppermute | solution.py:25
  64.7 20.3 %copy-start.5 = (bf16[3,3,128,128]{3,2,1,0:T(8,128)(2,1)S(1)}, bf16[3,3,128,128]{3,2,1,0:T(8,128)(2,1)}, u32[]{:S(2)}) copy-start(bf16[3,3,128,128]{3,2,1,0:T(8,128)(2,1)} %param.16) | copy-start | bytes 884740
  64.7 20.3 %copy-start.12 = (f32[128]{0:T(128)S(1)}, f32[128]{0:T(128)}, u32[]{:S(2)}) copy-start(f32[128]{0:T(128)} %param.17) | copy-start | bytes 1540
  64.8 6.6 %collective-permute-start.4 = (bf16[16,1,64,128]{3,0,2,1:T(8,128)(2,1)S(1)}, bf16[16,1,64,128]{3,0,2,1:T(8,128)(2,1)S(1)}, u32[]{:S(2)}, u32[]{:S(2)}) collective-permute-start(bf16[16,1,64,128]{3,0,2,1:T(8,128)(2,1)S(1)} %get-tuple-element.15), channel_id=1, source_target_pairs={{0,1},{1,2},{2,3},{3,4},{4,5},{5,6},{6,7},{8,9},{9,10},{10,11},{11... | collective-permute-start | bytes 786440 | tf_op jit(solution)/shard_map/ppermute | solution.py:24
  68.1 7.7 %collective-permute-start.5 = (bf16[16,1,64,128]{3,0,2,1:T(8,128)(2,1)S(1)}, bf16[16,1,64,128]{3,0,2,1:T(8,128)(2,1)S(1)}, u32[]{:S(2)}, u32[]{:S(2)}) collective-permute-start(bf16[16,1,64,128]{3,0,2,1:T(8,128)(2,1)S(1)} %get-tuple-element.16), channel_id=1, source_target_pairs={{1,0},{2,1},{3,2},{4,3},{5,4},{6,5},{7,6},{9,8},{10,9},{11,10},{12... | collective-permute-start | bytes 786440 | tf_op jit(solution)/shard_map/ppermute | solution.py:25
  75.8 5.4 %collective-permute-start.6 = (bf16[16,18,1,128]{3,0,2,1:T(8,128)(2,1)S(1)}, bf16[16,18,1,128]{3,0,2,1:T(8,128)(2,1)S(1)}, u32[]{:S(2)}, u32[]{:S(2)}) collective-permute-start(bf16[16,18,1,128]{3,0,2,1:T(8,128)(2,1)S(1)} %get-tuple-element.11), channel_id=1, source_target_pairs={{0,8},{8,16},{16,24},{1,9},{9,17},{17,25},{2,10},{10,18},{18,26},{... | collective-permute-start | bytes 221192 | tf_op jit(solution)/shard_map/ppermute | solution.py:24
  79.7 5.3 %collective-permute-start.7 = (bf16[16,18,1,128]{3,0,2,1:T(8,128)(2,1)S(1)}, bf16[16,18,1,128]{3,0,2,1:T(8,128)(2,1)S(1)}, u32[]{:S(2)}, u32[]{:S(2)}) collective-permute-start(bf16[16,18,1,128]{3,0,2,1:T(8,128)(2,1)S(1)} %get-tuple-element.12), channel_id=1, source_target_pairs={{8,0},{16,8},{24,16},{9,1},{17,9},{25,17},{10,2},{18,10},{26,18},{... | collective-permute-start | bytes 221192 | tf_op jit(solution)/shard_map/ppermute | solution.py:25
  95.3 19.8 %copy-start.4 = (bf16[4,4,128,256]{3,2,1,0:T(8,128)(2,1)S(1)}, bf16[4,4,128,256]{3,2,1,0:T(8,128)(2,1)}, u32[]{:S(2)}) copy-start(bf16[4,4,128,256]{3,2,1,0:T(8,128)(2,1)} %param.18) | copy-start | bytes 3145732
  95.3 19.8 %copy-start.9 = (f32[256]{0:T(256)S(1)}, f32[256]{0:T(256)}, u32[]{:S(2)}) copy-start(f32[256]{0:T(256)} %param.19) | copy-start | bytes 3076
  95.3 6.4 %collective-permute-start.8 = (bf16[16,1,64,128]{3,0,2,1:T(8,128)(2,1)S(1)}, bf16[16,1,64,128]{3,0,2,1:T(8,128)(2,1)S(1)}, u32[]{:S(2)}, u32[]{:S(2)}) collective-permute-start(bf16[16,1,64,128]{3,0,2,1:T(8,128)(2,1)S(1)} %get-tuple-element.13), channel_id=1, source_target_pairs={{0,1},{1,2},{2,3},{3,4},{4,5},{5,6},{6,7},{8,9},{9,10},{10,11},{11... | collective-permute-start | bytes 786440 | tf_op jit(solution)/shard_map/ppermute | solution.py:24
  98.5 7.7 %collective-permute-start.9 = (bf16[16,1,64,128]{3,0,2,1:T(8,128)(2,1)S(1)}, bf16[16,1,64,128]{3,0,2,1:T(8,128)(2,1)S(1)}, u32[]{:S(2)}, u32[]{:S(2)}) collective-permute-start(bf16[16,1,64,128]{3,0,2,1:T(8,128)(2,1)S(1)} %get-tuple-element.14), channel_id=1, source_target_pairs={{1,0},{2,1},{3,2},{4,3},{5,4},{6,5},{7,6},{9,8},{10,9},{11,10},{12... | collective-permute-start | bytes 786440 | tf_op jit(solution)/shard_map/ppermute | solution.py:25
  106.2 5.1 %collective-permute-start.10 = (bf16[16,18,1,128]{3,0,2,1:T(8,128)(2,1)S(1)}, bf16[16,18,1,128]{3,0,2,1:T(8,128)(2,1)S(1)}, u32[]{:S(2)}, u32[]{:S(2)}) collective-permute-start(bf16[16,18,1,128]{3,0,2,1:T(8,128)(2,1)S(1)} %get-tuple-element.9), channel_id=1, source_target_pairs={{0,8},{8,16},{16,24},{1,9},{9,17},{17,25},{2,10},{10,18},{18,26},{... | collective-permute-start | bytes 221192 | tf_op jit(solution)/shard_map/ppermute | solution.py:24
  109.8 28.0 %copy-start.3 = (bf16[3,3,256,256]{3,2,1,0:T(8,128)(2,1)S(1)}, bf16[3,3,256,256]{3,2,1,0:T(8,128)(2,1)}, u32[]{:S(2)}) copy-start(bf16[3,3,256,256]{3,2,1,0:T(8,128)(2,1)} %param.20) | copy-start | bytes 3538948
  109.8 28.0 %copy-start.10 = (f32[256]{0:T(256)S(1)}, f32[256]{0:T(256)}, u32[]{:S(2)}) copy-start(f32[256]{0:T(256)} %param.21) | copy-start | bytes 3076
  109.8 5.3 %collective-permute-start.11 = (bf16[16,18,1,128]{3,0,2,1:T(8,128)(2,1)S(1)}, bf16[16,18,1,128]{3,0,2,1:T(8,128)(2,1)S(1)}, u32[]{:S(2)}, u32[]{:S(2)}) collective-permute-start(bf16[16,18,1,128]{3,0,2,1:T(8,128)(2,1)S(1)} %get-tuple-element.10), channel_id=1, source_target_pairs={{8,0},{16,8},{24,16},{9,1},{17,9},{25,17},{10,2},{18,10},{26,18},{... | collective-permute-start | bytes 221192 | tf_op jit(solution)/shard_map/ppermute | solution.py:25
  119.9 6.5 %collective-permute-start.12 = (bf16[16,1,32,256]{3,0,2,1:T(8,128)(2,1)S(1)}, bf16[16,1,32,256]{3,0,2,1:T(8,128)(2,1)S(1)}, u32[]{:S(2)}, u32[]{:S(2)}) collective-permute-start(bf16[16,1,32,256]{3,0,2,1:T(8,128)(2,1)S(1)} %get-tuple-element.23), channel_id=1, source_target_pairs={{0,1},{1,2},{2,3},{3,4},{4,5},{5,6},{6,7},{8,9},{9,10},{10,11},{11... | collective-permute-start | bytes 786440 | tf_op jit(solution)/shard_map/ppermute | solution.py:24
  123.1 7.7 %collective-permute-start.13 = (bf16[16,1,32,256]{3,0,2,1:T(8,128)(2,1)S(1)}, bf16[16,1,32,256]{3,0,2,1:T(8,128)(2,1)S(1)}, u32[]{:S(2)}, u32[]{:S(2)}) collective-permute-start(bf16[16,1,32,256]{3,0,2,1:T(8,128)(2,1)S(1)} %get-tuple-element.24), channel_id=1, source_target_pairs={{1,0},{2,1},{3,2},{4,3},{5,4},{6,5},{7,6},{9,8},{10,9},{11,10},{12... | collective-permute-start | bytes 786440 | tf_op jit(solution)/shard_map/ppermute | solution.py:25
  130.9 3.1 %collective-permute-start.14 = (bf16[16,10,1,256]{3,0,2,1:T(8,128)(2,1)S(1)}, bf16[16,10,1,256]{3,0,2,1:T(8,128)(2,1)S(1)}, u32[]{:S(2)}, u32[]{:S(2)}) collective-permute-start(bf16[16,10,1,256]{3,0,2,1:T(8,128)(2,1)S(1)} %get-tuple-element.19), channel_id=1, source_target_pairs={{0,8},{8,16},{16,24},{1,9},{9,17},{17,25},{2,10},{10,18},{18,26},{... | collective-permute-start | bytes 245768 | tf_op jit(solution)/shard_map/ppermute | solution.py:24
  132.6 28.6 %copy-start.7 = (f32[320]{0:T(512)S(1)}, f32[320]{0:T(512)}, u32[]{:S(2)}) copy-start(f32[320]{0:T(512)} %param.23) | copy-start | bytes 3844
  132.6 5.2 %collective-permute-start.15 = (bf16[16,10,1,256]{3,0,2,1:T(8,128)(2,1)S(1)}, bf16[16,10,1,256]{3,0,2,1:T(8,128)(2,1)S(1)}, u32[]{:S(2)}, u32[]{:S(2)}) collective-permute-start(bf16[16,10,1,256]{3,0,2,1:T(8,128)(2,1)S(1)} %get-tuple-element.20), channel_id=1, source_target_pairs={{8,0},{16,8},{24,16},{9,1},{17,9},{25,17},{10,2},{18,10},{26,18},{... | collective-permute-start | bytes 245768 | tf_op jit(solution)/shard_map/ppermute | solution.py:25
  143.2 6.5 %collective-permute-start.16 = (bf16[16,1,32,256]{3,0,2,1:T(8,128)(2,1)S(1)}, bf16[16,1,32,256]{3,0,2,1:T(8,128)(2,1)S(1)}, u32[]{:S(2)}, u32[]{:S(2)}) collective-permute-start(bf16[16,1,32,256]{3,0,2,1:T(8,128)(2,1)S(1)} %get-tuple-element.21), channel_id=1, source_target_pairs={{0,1},{1,2},{2,3},{3,4},{4,5},{5,6},{6,7},{8,9},{9,10},{10,11},{11... | collective-permute-start | bytes 786440 | tf_op jit(solution)/shard_map/ppermute | solution.py:24
  146.4 7.7 %collective-permute-start.17 = (bf16[16,1,32,256]{3,0,2,1:T(8,128)(2,1)S(1)}, bf16[16,1,32,256]{3,0,2,1:T(8,128)(2,1)S(1)}, u32[]{:S(2)}, u32[]{:S(2)}) collective-permute-start(bf16[16,1,32,256]{3,0,2,1:T(8,128)(2,1)S(1)} %get-tuple-element.22), channel_id=1, source_target_pairs={{1,0},{2,1},{3,2},{4,3},{5,4},{6,5},{7,6},{9,8},{10,9},{11,10},{12... | collective-permute-start | bytes 786440 | tf_op jit(solution)/shard_map/ppermute | solution.py:25
  154.1 3.4 %collective-permute-start.18 = (bf16[16,10,1,256]{3,0,2,1:T(8,128)(2,1)S(1)}, bf16[16,10,1,256]{3,0,2,1:T(8,128)(2,1)S(1)}, u32[]{:S(2)}, u32[]{:S(2)}) collective-permute-start(bf16[16,10,1,256]{3,0,2,1:T(8,128)(2,1)S(1)} %get-tuple-element.17), channel_id=1, source_target_pairs={{0,8},{8,16},{16,24},{1,9},{9,17},{17,25},{2,10},{10,18},{18,26},{... | collective-permute-start | bytes 245768 | tf_op jit(solution)/shard_map/ppermute | solution.py:24
  155.8 27.1 %copy-start.2 = (bf16[3,3,320,320]{3,2,1,0:T(8,128)(2,1)S(1)}, bf16[3,3,320,320]{3,2,1,0:T(8,128)(2,1)}, u32[]{:S(2)}) copy-start(bf16[3,3,320,320]{3,2,1,0:T(8,128)(2,1)} %param.24) | copy-start | bytes 5529604
  155.8 27.0 %copy-start.8 = (f32[320]{0:T(512)S(1)}, f32[320]{0:T(512)}, u32[]{:S(2)}) copy-start(f32[320]{0:T(512)} %param.25) | copy-start | bytes 3844
  155.9 5.3 %collective-permute-start.19 = (bf16[16,10,1,256]{3,0,2,1:T(8,128)(2,1)S(1)}, bf16[16,10,1,256]{3,0,2,1:T(8,128)(2,1)S(1)}, u32[]{:S(2)}, u32[]{:S(2)}) collective-permute-start(bf16[16,10,1,256]{3,0,2,1:T(8,128)(2,1)S(1)} %get-tuple-element.18), channel_id=1, source_target_pairs={{8,0},{16,8},{24,16},{9,1},{17,9},{25,17},{10,2},{18,10},{26,18},{... | collective-permute-start | bytes 245768 | tf_op jit(solution)/shard_map/ppermute | solution.py:25
  165.8 5.8 %collective-permute-start.20 = (bf16[16,1,16,320]{3,0,2,1:T(8,128)(2,1)S(1)}, bf16[16,1,16,320]{3,0,2,1:T(8,128)(2,1)S(1)}, u32[]{:S(2)}, u32[]{:S(2)}) collective-permute-start(bf16[16,1,16,320]{3,0,2,1:T(8,128)(2,1)S(1)} %get-tuple-element.27), channel_id=1, source_target_pairs={{0,1},{1,2},{2,3},{3,4},{4,5},{5,6},{6,7},{8,9},{9,10},{10,11},{11... | collective-permute-start | bytes 491528 | tf_op jit(solution)/shard_map/ppermute | solution.py:24
  169.0 7.0 %collective-permute-start.21 = (bf16[16,1,16,320]{3,0,2,1:T(8,128)(2,1)S(1)}, bf16[16,1,16,320]{3,0,2,1:T(8,128)(2,1)S(1)}, u32[]{:S(2)}, u32[]{:S(2)}) collective-permute-start(bf16[16,1,16,320]{3,0,2,1:T(8,128)(2,1)S(1)} %get-tuple-element.28), channel_id=1, source_target_pairs={{1,0},{2,1},{3,2},{4,3},{5,4},{6,5},{7,6},{9,8},{10,9},{11,10},{12... | collective-permute-start | bytes 491528 | tf_op jit(solution)/shard_map/ppermute | solution.py:25
  176.1 3.1 %collective-permute-start.22 = (bf16[16,6,1,320]{3,0,2,1:T(8,128)(2,1)S(1)}, bf16[16,6,1,320]{3,0,2,1:T(8,128)(2,1)S(1)}, u32[]{:S(2)}, u32[]{:S(2)}) collective-permute-start(bf16[16,6,1,320]{3,0,2,1:T(8,128)(2,1)S(1)} %get-tuple-element.25), channel_id=1, source_target_pairs={{0,8},{8,16},{16,24},{1,9},{9,17},{17,25},{2,10},{10,18},{18,26},{... | collective-permute-start | bytes 184328 | tf_op jit(solution)/shard_map/ppermute | solution.py:24
  177.8 5.1 %collective-permute-start.23 = (bf16[16,6,1,320]{3,0,2,1:T(8,128)(2,1)S(1)}, bf16[16,6,1,320]{3,0,2,1:T(8,128)(2,1)S(1)}, u32[]{:S(2)}, u32[]{:S(2)}) collective-permute-start(bf16[16,6,1,320]{3,0,2,1:T(8,128)(2,1)S(1)} %get-tuple-element.26), channel_id=1, source_target_pairs={{8,0},{16,8},{24,16},{9,1},{17,9},{25,17},{10,2},{18,10},{26,18},{... | collective-permute-start | bytes 184328 | tf_op jit(solution)/shard_map/ppermute | solution.py:25
where the time goes:
time: 189 us; the launch traced here: 187 us
  waiting for transfers between devices  60.6 us (32%)
  starting transfers between devices  57.7 us (31%)
  matrix products  45.8 us (24%)
  local copies, waits for them, and re-layouts  21.6 us (11%)
    ppermute x12, waiting for transfers between devices, add_halo(): from_next = lax.ppermute(head_edge, axis_name, to_prev)  50.1 us
    conv_general_dilated x6, matrix products, conv_relu(): lax.conv_general_dilated(padded, weight, (stride, stride), 'VALID', dimen...  45.8 us
    ppermute x12, starting transfers between devices, add_halo(): from_prev = lax.ppermute(tail_edge, axis_name, to_next)  37.1 us
    ppermute x12, starting transfers between devices, add_halo(): from_next = lax.ppermute(head_edge, axis_name, to_prev)  20.6 us
    unnamed x27, local copies, waits for them, and re-layouts  19 us
    ppermute x12, waiting for transfers between devices, add_halo(): from_prev = lax.ppermute(tail_edge, axis_name, to_next)  10.5 us
  transfers between devices with their start and end apart: 24, of which 21 were waited for; matrix products, arithmetic and copies ran while one was open for 0% of the time, Pallas kernels for 0%

commit v1 on v0

v1 whole, which is shorter than its diff:
```python
import functools

import jax
import jax.numpy as jnp
from jax import lax
from jax.experimental import pallas as pl
from jax.experimental.pallas import tpu as pltpu
from jax.sharding import PartitionSpec as P

BY_LAST = (((1,), (1,)), ((), ()))
BF = jnp.bfloat16
F32 = jnp.float32
LANES = 128
TILE = 2 * LANES
PITCH = 136


def _encoder_kernel(dims, img, wd1, bd1, wc1, bc1, wd2, bd2, wc2, bc2, wd3, bd3, wc3, bc3, out,
                    raw, xt, y1, z1, y2, z2, y3, st0, st1, st2,
                    vwd1, vwc1, vwd2, vwc2, vwd3, vwc3, wp1, wp2, wp6,
                    vb1, vb2, vb3, vb4, vb5, vb6,
                    raw_sem, w_sem, rh_send, rh_recv, xc_send, xc_recv,
                    row_send, row_recv, cor_send, cor_recv, col_send, col_recv):
    row_len, col_len = dims
    nimg = img.shape[0]
    my_row = lax.axis_index('row')
    my_col = lax.axis_index('col')
    up, down = my_row > 0, my_row < row_len - 1
    left, right = my_col > 0, my_col < col_len - 1

    def both(a, b):
        return jnp.logical_and(a, b)

    near = [(up, -1, 0), (down, 1, 0), (left, 0, -1), (right, 0, 1)]
    near += [(both(v[0], g[0]), v[1], g[2]) for v in near[:2] for g in near[2:]]

    def dev(dr, dc):
        return {'row': my_row + dr, 'col': my_col + dc}

    def raw_copy(k):
        return pltpu.make_async_copy(img.at[:, pl.ds(2 * k - 1, 2)], raw.at[k], raw_sem.at[k])

    last = raw.shape[0] - 1
    mid = last // 2
    first_copy = pltpu.make_async_copy(img.at[:, pl.ds(0, 1)], raw.at[0, :, pl.ds(1, 1)], raw_sem.at[0])
    last_copy = pltpu.make_async_copy(img.at[:, pl.ds(2 * last - 1, 1)], raw.at[last, :, pl.ds(0, 1)], raw_sem.at[last])
    order = []
    for t in range(last - 1):
        h = (t + 1) // 2
        order.append(mid - h if t % 2 else mid + h)
    for k in order[:3]:
        raw_copy(k).start()
    weights = [(wd1, vwd1), (wc1, vwc1), (wd2, vwd2), (wc2, vwc2), (wd3, vwd3), (wc3, vwc3),
               (bd1, vb1), (bc1, vb2), (bd2, vb3), (bc2, vb4), (bd3, vb5), (bc3, vb6)]
    wcopies = [pltpu.make_async_copy(s, d, w_sem.at[i]) for i, (s, d) in enumerate(weights)]
    for i in (0, 6, 1, 7):
        wcopies[i].start()
    for k in order[3:]:
        raw_copy(k).start()
    first_copy.start()
    last_copy.start()
    for i in (2, 8, 3, 9, 4, 10, 5, 11):
        wcopies[i].start()

    barrier = pltpu.get_barrier_semaphore()
    for there, dr, dc in near:
        @pl.when(there)
        def _(dr=dr, dc=dc):
            pl.semaphore_signal(barrier, inc=1, device_id=dev(dr, dc), device_id_type=pl.DeviceIdType.MESH)
    nu, nd, nl, nr = [jnp.where(x, 1, 0) for x in (up, down, left, right)]
    pl.semaphore_wait(barrier, (1 + nu + nd) * (1 + nl + nr) - 1)

    def raw_send(s):
        if s == 0:
            return pltpu.make_async_remote_copy(img.at[:, pl.ds(0, 1)], raw.at[last, :, pl.ds(1, 1)],
                                                rh_send.at[0], rh_recv.at[0], device_id=dev(-1, 0), device_id_type=pl.DeviceIdType.MESH)
        return pltpu.make_async_remote_copy(img.at[:, pl.ds(2 * last - 1, 1)], raw.at[0, :, pl.ds(0, 1)],
                                            rh_send.at[1], rh_recv.at[1], device_id=dev(1, 0), device_id_type=pl.DeviceIdType.MESH)

    for there, s in zip((up, down), range(2)):
        @pl.when(there)
        def _(s=s):
            raw_send(s).start()

    def zero(ref):
        ref[...] = jnp.zeros(ref.shape, ref.dtype)

    def wide(ref, h):
        u = ref.shape[1] - 2
        return dict(ref=ref, h=h, hl=(0, 1), first=(1, 0), last=(u, 1), hr=(u + 1, 0), real=pl.ds(1, u))

    def flat(ref, h):
        w = ref.shape[1] - 2
        return dict(ref=ref, h=h, hl=(0,), first=(1,), last=(w,), hr=(w + 1,), real=pl.ds(1, w))

    bufs = [wide(y1, y1.shape[0] - 2), wide(z1, z1.shape[0] - 2), flat(y2, y2.shape[0] - 2), wide(z2, z2.shape[0] - 2),
            flat(y3, y3.shape[0] - 2)]

    for b in bufs:
        ref, h = b['ref'], b['h']

        @pl.when(jnp.logical_not(up))
        def _(ref=ref):
            zero(ref.at[0])

        @pl.when(jnp.logical_not(down))
        def _(ref=ref, h=h):
            zero(ref.at[h + 1])

        @pl.when(jnp.logical_not(left))
        def _(ref=ref, b=b, h=h):
            for r in range(h + 2):
                zero(ref.at[(r,) + b['hl']])

        @pl.when(jnp.logical_not(right))
        def _(ref=ref, b=b, h=h):
            for r in range(h + 2):
                zero(ref.at[(r,) + b['hr']])

    @pl.when(jnp.logical_not(up))
    def _():
        for n in range(nimg):
            zero(raw.at[0, n, 0])

    @pl.when(jnp.logical_not(down))
    def _():
        for n in range(nimg):
            zero(raw.at[last, n, 1])

    xu = xt.shape[1] - 2

    @pl.when(jnp.logical_not(left))
    def _():
        for k in range(last + 1):
            zero(xt.at[k, 0, 3])

    @pl.when(jnp.logical_not(right))
    def _():
        for k in range(last + 1):
            zero(xt.at[k, xu + 1, 0])

    def row_copy(i, s):
        b = bufs[i]
        ref, h = b['ref'], b['h']
        src, dst, dr = (1, h + 1, -1) if s == 0 else (h, 0, 1)
        return pltpu.make_async_remote_copy(ref.at[src, b['real']], ref.at[dst, b['real']], row_send.at[i, s], row_recv.at[i, s],
                                            device_id=dev(dr, 0), device_id_type=pl.DeviceIdType.MESH)

    def corner_copy(i, s):
        b = bufs[i]
        ref, h = b['ref'], b['h']
        dr, dc = near[4 + s][1:]
        src = (1 if dr < 0 else h,) + (b['first'] if dc < 0 else b['last'])
        dst = (h + 1 if dr < 0 else 0,) + (b['hr'] if dc < 0 else b['hl'])
        return pltpu.make_async_remote_copy(ref.at[src], ref.at[dst], cor_send.at[i, s], cor_recv.at[i, s],
                                            device_id=dev(dr, dc), device_id_type=pl.DeviceIdType.MESH)

    def col_copy(i, r, s):
        b = bufs[i]
        ref = b['ref']
        src, dst, dc = (b['first'], b['hr'], -1) if s == 0 else (b['last'], b['hl'], 1)
        return pltpu.make_async_remote_copy(ref.at[(r + 1,) + src], ref.at[(r + 1,) + dst], col_send.at[i, r, s], col_recv.at[i, r, s],
                                            device_id=dev(0, dc), device_id_type=pl.DeviceIdType.MESH)

    sides = ((left, 0), (right, 1))
    from_sides = ((right, 0), (left, 1))

    def each(cases, act):
        for there, s in cases:
            @pl.when(there)
            def _(s=s):
                act(s)

    def send_cols(i, r):
        each(sides, lambda s: col_copy(i, r, s).start())

    def wait_cols(i, r):
        each(from_sides, lambda s: col_copy(i, r, s).wait_recv())

    ends = list(zip((up, down), range(2)))
    from_ends = list(zip((down, up), range(2)))
    corners = [(x[0], s) for s, x in enumerate(near[4:])]
    from_corners = [(x[0], s) for s, x in enumerate(near[:3:-1])]

    def send_rows(i):
        each(ends, lambda s: row_copy(i, s).start())
        each(corners, lambda s: corner_copy(i, s).start())

    def wait_rows(i):
        each(from_ends, lambda s: row_copy(i, s).wait_recv())
        each(from_corners, lambda s: corner_copy(i, s).wait_recv())

    def xcol_copy(k, s):
        src, dst, dc = ((1, 0), (xu + 1, 0), -1) if s == 0 else ((xu, 3), (0, 3), 1)
        return pltpu.make_async_remote_copy(xt.at[(k,) + src], xt.at[(k,) + dst], xc_send.at[k, s], xc_recv.at[k, s],
                                            device_id=dev(0, dc), device_id_type=pl.DeviceIdType.MESH)

    def send_xcols(k):
        each(sides, lambda s: xcol_copy(k, s).start())

    def wait_xcols(k):
        each(from_sides, lambda s: xcol_copy(k, s).wait_recv())

    for i in (0, 1, 6, 7):
        wcopies[i].wait()
    zb = jnp.zeros((64, LANES), BF)
    for dk in range(2):
        for dc in range(3):
            for cpar in range(2):
                for rpar in range(2):
                    r0 = (dk * 3 + dc) * TILE + (cpar * 2 + rpar) * 64
                    for j in range(2):
                        q = 2 * (dc - j) + cpar
                        wp1[pl.ds(r0, 64), pl.ds(j * LANES, LANES)] = vwd1[2 * dk + rpar, q] if 0 <= q < 4 else zb
    zc = jnp.zeros((LANES, LANES), BF)
    for p in range(3):
        for s in range(4):
            for j in range(2):
                q = s - j
                wp2[pl.ds((p * 4 + s) * LANES, LANES), pl.ds(j * LANES, LANES)] = vwc1[p, q] if 0 <= q < 3 else zc

    eye = (lax.broadcasted_iota(jnp.int32, (LANES, LANES), 0) == lax.broadcasted_iota(jnp.int32, (LANES, LANES), 1)).astype(F32).astype(BF)

    def transpose_in(k, st):
        for s in range(nimg // 2):
            rhs = raw[k, pl.ds(2 * s, 2)].reshape(TILE, LANES)
            t = lax.dot_general(eye, rhs, BY_LAST, preferred_element_type=F32)
            st[pl.ds(2 * s * PITCH, LANES), :] = t[:, :LANES]
            st[pl.ds((2 * s + 1) * PITCH, LANES), :] = t[:, LANES:]

    def transpose_out(k, st):
        for c in range(4 * xu):
            xt[k, 1 + c // 4, c % 4] = st[pl.ds(c, nimg, stride=PITCH), :].astype(BF)

    def middle_out(t):
        h = (t + 1) // 2
        return mid + h * (1 - 2 * (t % 2))

    def take_three(it, carry):
        ks = [middle_out(3 * it + d) for d in range(3)]
        sts = [st0, st1, st2]
        for k in ks:
            raw_copy(k).wait()
        for k, st in zip(ks, sts):
            transpose_in(k, st)
        for k, st in zip(ks, sts):
            transpose_out(k, st)
        for k in ks:
            send_xcols(k)
        return carry

    lax.fori_loop(0, (last - 1) // 3, take_three, 0)

    def take_edges():
        first_copy.wait()
        last_copy.wait()

        each(from_ends, lambda s: raw_send(s).wait_recv())
        transpose_in(0, st0)
        transpose_in(last, st1)
        transpose_out(0, st0)
        transpose_out(last, st1)
        send_xcols(0)
        send_xcols(last)

    def finish(acc, bias):
        return jnp.maximum(acc + bias, 0.0).astype(BF)

    def put_pairs(ref, i, v):
        for j in range(2):
            ref[i + 1, pl.ds(1, pairs), j] = v[:, j * LANES:(j + 1) * LANES].reshape(pairs, nimg, LANES)

    def rows_of(ref, idx, w):
        v = ref[idx]
        return v.reshape(w * nimg, v.shape[-1])

    pairs = y1.shape[1] - 2
    bias1 = jnp.concatenate([vb1[...], vb1[...]], axis=-1)
    h1 = y1.shape[0] - 2

    def down1(t, carry):
        a = h1 // 2 - 1 - t

        @pl.when(t == 0)
        def _():
            wait_xcols(mid)

        @pl.when(t == 4)
        def _():
            take_edges()
        wait_xcols(a)
        wait_xcols(last - a)
        for i in (a, h1 - 1 - a):
            parts = []
            for dk in range(2):
                for p in range(3, 9):
                    parts.append(rows_of(xt, (i + dk, pl.ds(p // 4, pairs), p % 4), pairs))
            acc = jnp.dot(jnp.concatenate(parts, axis=-1), wp1[...], preferred_element_type=F32)
            v = finish(acc, bias1)
            put_pairs(y1, i, v)
        send_cols(0, a)
        send_cols(0, h1 - 1 - a)
        return carry

    lax.fori_loop(0, h1 // 2, down1, 0)
    send_rows(0)

    def wait_conv(i, a, h):
        @pl.when(a == h // 2 - 1)
        def _():
            wait_cols(i, a)
            wait_cols(i, h - 1 - a)

        @pl.when(a > 0)
        def _():
            wait_cols(i, a - 1)
            wait_cols(i, h - a)

        @pl.when(a == 0)
        def _():
            wait_rows(i)

    def wait_down(i, a, h):
        hs = 2 * h

        @pl.when(a == h // 2 - 1)
        def _():
            wait_cols(i, 2 * a + 1)
            wait_cols(i, hs - 2 - 2 * a)
        wait_cols(i, 2 * a)
        wait_cols(i, hs - 1 - 2 * a)

        @pl.when(a > 0)
        def _():
            wait_cols(i, 2 * a - 1)
            wait_cols(i, hs - 2 * a)

        @pl.when(a == 0)
        def _():
            wait_rows(i)

    bias2 = jnp.concatenate([vb2[...], vb2[...]], axis=-1)

    def conv1(t, carry):
        a = h1 // 2 - 1 - t
        wait_conv(0, a, h1)
        for i in (a, h1 - 1 - a):
            parts = []
            for p in range(3):
                for s in range(1, 5):
                    parts.append(rows_of(y1, (i + p, pl.ds(s // 2, pairs), s % 2), pairs))
            acc = jnp.dot(jnp.concatenate(parts, axis=-1), wp2[...], preferred_element_type=F32)
            v = finish(acc, bias2)
            put_pairs(z1, i, v)
        send_cols(1, a)
        send_cols(1, h1 - 1 - a)
        return carry

    lax.fori_loop(0, h1 // 2, conv1, 0)
    send_rows(1)

    h2 = y2.shape[0] - 2
    w2 = y2.shape[1] - 2
    for i in (2, 8):
        wcopies[i].wait()

    def down2(t, carry):
        a = h2 // 2 - 1 - t
        wait_down(1, a, h2)
        for i in (a, h2 - 1 - a):
            parts = []
            for p in range(4):
                for s in range(1, 5):
                    parts.append(rows_of(z1, (2 * i + p, pl.ds(s // 2, w2), s % 2), w2))
            acc = jnp.dot(jnp.concatenate(parts, axis=-1), vwd2[...].reshape(16 * LANES, TILE), preferred_element_type=F32)
            y2[i + 1, pl.ds(1, w2)] = finish(acc, vb3[...]).reshape(w2, nimg, TILE)
        send_cols(2, a)
        send_cols(2, h2 - 1 - a)
        return carry

    lax.fori_loop(0, h2 // 2, down2, 0)
    send_rows(2)
    for i in (3, 9):
        wcopies[i].wait()

    def conv2(t, carry):
        a = h2 // 2 - 1 - t
        wait_conv(2, a, h2)
        for i in (a, h2 - 1 - a):
            parts = []
            for p in range(3):
                for q in range(3):
                    parts.append(rows_of(y2, (i + p, pl.ds(q, w2)), w2))
            acc = jnp.dot(jnp.concatenate(parts, axis=-1), vwc2[...].reshape(9 * TILE, TILE), preferred_element_type=F32)
            v = finish(acc, vb4[...]).reshape(w2 // 2, 2, nimg, TILE)
            z2[i + 1, pl.ds(1, w2 // 2), 0] = v[:, 0]
            z2[i + 1, pl.ds(1, w2 // 2), 1] = v[:, 1]
        send_cols(3, a)
        send_cols(3, h2 - 1 - a)
        return carry

    lax.fori_loop(0, h2 // 2, conv2, 0)
    send_rows(3)

    h3 = y3.shape[0] - 2
    w3 = y3.shape[1] - 2
    ch3 = out.shape[-1]
    for i in (4, 10, 5, 11):
        wcopies[i].wait()
    wp6[...] = jnp.zeros(wp6.shape, BF)
    for p in range(3):
        for q in range(3):
            wp6[p * 3 + q, pl.ds(0, ch3), :] = vwc3[p, q]

    def down3(t, carry):
        a = h3 // 2 - 1 - t
        wait_down(3, a, h3)
        ii = (a, h3 - 1 - a)
        acc = None
        for p in range(4):
            for s in range(1, 5):
                lhs = jnp.concatenate([rows_of(z2, (2 * i + p, pl.ds(s // 2, w3), s % 2), w3) for i in ii], axis=0)
                d = lax.dot_general(lhs, vwd3[p, s - 1], BY_LAST, preferred_element_type=F32)
                acc = d if acc is None else acc + d
        v = finish(acc, vb5[...])
        v = jnp.concatenate([v, jnp.zeros((v.shape[0], y3.shape[-1] - ch3), BF)], axis=-1)
        for n, i in enumerate(ii):
            y3[i + 1, pl.ds(1, w3)] = v[n * w3 * nimg:(n + 1) * w3 * nimg].reshape(w3, nimg, y3.shape[-1])
        send_cols(4, a)
        send_cols(4, h3 - 1 - a)
        return carry

    lax.fori_loop(0, h3 // 2, down3, 0)
    send_rows(4)

    def conv3(t, carry):
        a = h3 // 2 - 1 - t
        wait_conv(4, a, h3)
        ii = (a, h3 - 1 - a)
        parts = []
        for p in range(3):
            for q in range(3):
                parts.append(jnp.concatenate([rows_of(y3, (i + p, pl.ds(q, w3)), w3) for i in ii], axis=0))
        acc = jnp.dot(jnp.concatenate(parts, axis=-1), wp6[...].reshape(9 * wp6.shape[1], ch3), preferred_element_type=F32)
        v = finish(acc, vb6[...])
        for n, i in enumerate(ii):
            out[i] = v[n * w3 * nimg:(n + 1) * w3 * nimg].reshape(w3, nimg, ch3)
        return carry

    lax.fori_loop(0, h3 // 2, conv3, 0)

    each(ends, lambda s: raw_send(s).wait_send())

    def drain(make, count):
        def one(r, carry):
            make(r).wait_send()
            return carry
        lax.fori_loop(0, count, one, 0)

    each(sides, lambda s: drain(lambda k: xcol_copy(k, s), last + 1))
    for i, b in enumerate(bufs):
        each(ends, lambda s: row_copy(i, s).wait_send())
        each(corners, lambda s: corner_copy(i, s).wait_send())
        each(sides, lambda s: drain(lambda r: col_copy(i, r, s), b['h']))


def solution(mesh):
    dims = (mesh.shape['row'], mesh.shape['col'])

    def local_encoder(images, w_down1, b_down1, w_conv1, b_conv1, w_down2, b_down2, w_conv2, b_conv2, w_down3, b_down3, w_conv3, b_conv3):
        n, h, w, c = images.shape
        img = jnp.transpose(images, (0, 1, 3, 2))
        wd3 = jnp.transpose(w_down3, (0, 1, 3, 2))
        c1, c2, c3 = w_conv1.shape[-1], w_conv2.shape[-1], w_conv3.shape[-1]
        c3p = pl.cdiv(c3, LANES) * LANES
        hbm = pl.BlockSpec(memory_space=pl.ANY)
        dma = pltpu.SemaphoreType.DMA
        hh, hq, he = h // 2, h // 4, h // 8
        wq, we = w // 4, w // 8
        kk = hh + 1
        scratch = [
            pltpu.VMEM((kk, n, 2, c, w), BF),
            pltpu.VMEM((kk, wq + 2, 4, n, 2 * c), BF),
            pltpu.VMEM((hh + 2, wq + 2, 2, n, c1), BF),
            pltpu.VMEM((hh + 2, wq + 2, 2, n, c1), BF),
            pltpu.VMEM((hq + 2, wq + 2, n, c2), BF),
            pltpu.VMEM((hq + 2, we + 2, 2, n, c2), BF),
            pltpu.VMEM((he + 2, we + 2, n, c3p), BF),
        ] + [pltpu.VMEM((n * PITCH, LANES), F32)] * 3 + [
            pltpu.VMEM(x.shape, BF) for x in (w_down1, w_conv1, w_down2, w_conv2, wd3, w_conv3)
        ] + [
            pltpu.VMEM((6 * TILE, TILE), BF),
            pltpu.VMEM((6 * TILE, TILE), BF),
            pltpu.VMEM((9, c3p, c3), BF),
        ] + [pltpu.VMEM((1, k), F32) for k in (c1, c1, c2, c2, c3, c3)] + [
            dma(d) for d in ((kk,), (12,), (2,), (2,), (kk, 2), (kk, 2), (5, 2), (5, 2), (5, 4), (5, 4), (5, hh, 2), (5, hh, 2))
        ]
        biases = [b.reshape(1, -1) for b in (b_down1, b_conv1, b_down2, b_conv2, b_down3, b_conv3)]
        feats = pl.pallas_call(
            functools.partial(_encoder_kernel, dims),
            out_shape=jax.ShapeDtypeStruct((he, we, n, c3), BF),
            in_specs=[hbm] * 13,
            out_specs=pl.BlockSpec(memory_space=pltpu.VMEM),
            scratch_shapes=scratch,
            compiler_params=pltpu.CompilerParams(collective_id=0, has_side_effects=True, vmem_limit_bytes=62 * 1024 * 1024),
        )(img, w_down1, biases[0], w_conv1, biases[1], w_down2, biases[2], w_conv2, biases[3], wd3, biases[4], w_conv3, biases[5])
        return jnp.transpose(feats, (2, 0, 1, 3))

    tile_spec = P('batch', 'row', 'col', None)
    return jax.shard_map(local_encoder, mesh=mesh, in_specs=(tile_spec,) + (P(),) * 12, out_specs=tile_spec, check_vma=False)
```

time: 189 us -> 69.9 us (0.37)
  Pallas kernels: 0 us -> 65.1 us
  waiting for transfers between devices: 60.6 us -> 0 us
  starting transfers between devices: 57.7 us -> 0 us
  matrix products: 45.8 us -> 0 us
  local copies, waits for them, and re-layouts: 21.6 us -> 4.7 us
    pallas_call x0 -> x1, Pallas kernels: none -> 65.1 us  [local_encoder(): pl.pallas_call(functools.partial(_encoder_kernel, dims), out_shape=jax.Sh...]
    ppermute x24 -> x0, waiting for transfers between devices: 60.6 us -> none  [the longest x12 50.1 us: add_halo(): from_next = lax.ppermute(head_edge, axis_name, to_prev)]
    ppermute x24 -> x0, starting transfers between devices: 57.7 us -> none  [the longest x12 37.1 us: add_halo(): from_prev = lax.ppermute(tail_edge, axis_name, to_next)]
    conv_general_dilated x6 -> x0, matrix products: 45.8 us -> none  [conv_relu(): lax.conv_general_dilated(padded, weight, (stride, stride), 'VALID', dimen...]
    unnamed x27 -> x0, local copies, waits for them, and re-layouts: 19 us -> none
    reshape x0 -> x2, local copies, waits for them, and re-layouts: none -> 2.5 us  [local_encoder(): b.reshape(1, -1)]
    transpose x0 -> x1, local copies, waits for them, and re-layouts: none -> 2.2 us  [local_encoder(): return jnp.transpose(feats, (2, 0, 1, 3))]
  transfers between devices with their start and end apart: 24 -> 0, of which waited for: 21 -> 0; matrix products, arithmetic and copies ran while one was open for 0% -> 0% of each run, Pallas kernels for 0% -> 0%
where the time goes in v1:
time: 69.9 us; the launch traced here: 69.8 us
  Pallas kernels  65.1 us (93%)
  local copies, waits for them, and re-layouts  4.7 us (7%)
    pallas_call x1, Pallas kernels, local_encoder(): pl.pallas_call(functools.partial(_encoder_kernel, dims), out_shape=jax.Sh...  65.1 us
    reshape x2, local copies, waits for them, and re-layouts, local_encoder(): b.reshape(1, -1)  2.5 us
    transpose x1, local copies, waits for them, and re-layouts, local_encoder(): return jnp.transpose(feats, (2, 0, 1, 3))  2.2 us

profile of v1, /device:TPU:97, one launch (start us, length us, event | category | flops | bytes accessed | tf_op | source)
XLA Modules:
  0.0 69.8 jit_solution(9972672136136664552)
XLA Ops:
  0.0 1.2 %reshape.22.bd3 = f32[1,320]{1,0:T(1,128)} reshape(f32[320]{0:T(512)} %param.23) | data formatting | bytes 2560 | tf_op jit(solution)/shard_map/reshape | solution.py:498
  1.2 1.3 %reshape.23.bc3 = f32[1,320]{1,0:T(1,128)} reshape(f32[320]{0:T(512)} %param.25) | data formatting | bytes 2560 | tf_op jit(solution)/shard_map/reshape | solution.py:498
  2.5 65.1 %shard_map.127 = bf16[4,16,16,320]{3,2,1,0:T(8,128)(2,1)} custom-call(bf16[16,32,64,128]{3,2,1,0:T(8,128)(2,1)} %bitcast.7, bf16[4,4,64,128]{3,2,1,0:T(8,128)(2,1)} %wd1.1, f32[1,128]{1,0:T(1,128)} %bitcast.12, bf16[3,3,128,128]{3,2,1,0:T(8,128)(2,1)} %wc1.1, f32[1,128]{1,0:T(1,128)} %bitcast.13, bf16[4,4,128,256]{3,2,1,0:T(8,128)(2,1)} %wd2.1, ...), custom_call_target="tpu_custom_call" | custom-call | tf_op jit(solution)/shard_map/pallas_call | solution.py:499
  67.6 2.2 %copy.14 = bf16[16,4,16,320]{3,2,1,0:T(8,128)(2,1)} copy(bf16[16,4,16,320]{3,0,2,1:T(8,128)(2,1)} %bitcast.8) | data formatting | bytes 1310720 | tf_op jit(solution)/shard_map/transpose | solution.py:507

commit v2 on v1

--- a/solution.py
+++ b/solution.py
@@ -12,7 +12,7 @@
 F32 = jnp.float32
 LANES = 128
 TILE = 2 * LANES
-PITCH = 136
+PITCH = 129
 
 
 def _encoder_kernel(dims, img, wd1, bd1, wc1, bc1, wd2, bd2, wc2, bc2, wd3, bd3, wc3, bc3, out,
@@ -48,14 +48,12 @@
     for t in range(last - 1):
         h = (t + 1) // 2
         order.append(mid - h if t % 2 else mid + h)
-    for k in order[:3]:
-        raw_copy(k).start()
     weights = [(wd1, vwd1), (wc1, vwc1), (wd2, vwd2), (wc2, vwc2), (wd3, vwd3), (wc3, vwc3),
-               (bd1, vb1), (bc1, vb2), (bd2, vb3), (bc2, vb4), (bd3, vb5), (bc3, vb6)]
+               *((x, v.at[0]) for x, v in zip((bd1, bc1, bd2, bc2, bd3, bc3), (vb1, vb2, vb3, vb4, vb5, vb6)))]
     wcopies = [pltpu.make_async_copy(s, d, w_sem.at[i]) for i, (s, d) in enumerate(weights)]
     for i in (0, 6, 1, 7):
         wcopies[i].start()
-    for k in order[3:]:
+    for k in order:
         raw_copy(k).start()
     first_copy.start()
     last_copy.start()
@@ -274,22 +272,86 @@
         v = ref[idx]
         return v.reshape(w * nimg, v.shape[-1])
 
+    def wait_pair(i, a, h):
+        wait_cols(i, a)
+        wait_cols(i, h - 1 - a)
+
+    def wait_conv(i, t, a, h, e):
+        n = h // 2
+
+        @pl.when(t == (0 if e else 1))
+        def _():
+            wait_pair(i, n - 1, h)
+
+        @pl.when(jnp.logical_or(t < e, a >= 3))
+        def _():
+            wait_pair(i, a - 1, h)
+
+        @pl.when(t == e)
+        def _():
+            for s in range(min(2, n - e - 1)):
+                wait_pair(i, s, h)
+            wait_rows(i)
+
+    def wait_down(i, t, a, h, e):
+        n = h // 2
+
+        @pl.when(t == (0 if e else 1))
+        def _():
+            wait_pair(i, h - 1, 2 * h)
+
+        @pl.when(jnp.logical_or(t < e, a >= 2))
+        def _():
+            wait_pair(i, 2 * a, 2 * h)
+            wait_pair(i, 2 * a - 1, 2 * h)
+
+        @pl.when(t == e)
+        def _():
+            for s in range(min(3, 2 * (n - e) - 1)):
+                wait_pair(i, s, 2 * h)
+            wait_rows(i)
+
+    def send(i, t, a, h, e):
+        send_cols(i, a)
+        send_cols(i, h - 1 - a)
+
+        @pl.when(t == e)
+        def _():
+            send_rows(i)
+
+    def step_of(t, n, e):
+        if not e:
+            return lax.rem(n - t, n)
+        past = (t + n - 1 - e) // n
+        return n - 1 - t + past - (n - 1 - e) * ((t + n - e) // n - past)
+
     pairs = y1.shape[1] - 2
     bias1 = jnp.concatenate([vb1[...], vb1[...]], axis=-1)
     h1 = y1.shape[0] - 2
 
+    e1 = 4
+
     def down1(t, carry):
-        a = h1 // 2 - 1 - t
+        a = step_of(t, h1 // 2, e1)
 
         @pl.when(t == 0)
         def _():
             wait_xcols(mid)
 
-        @pl.when(t == 4)
+        @pl.when(t == 1)
         def _():
             take_edges()
-        wait_xcols(a)
-        wait_xcols(last - a)
+
+        @pl.when(jnp.logical_or(t < e1, a >= 2))
+        def _():
+            wait_xcols(a)
+            wait_xcols(last - a)
+
+        @pl.when(t == e1)
+        def _():
+            for k in (0, 1):
+                wait_xcols(k)
+                wait_xcols(last - k)
         for i in (a, h1 - 1 - a):
             parts = []
             for dk in range(2):
@@ -298,52 +360,16 @@
             acc = jnp.dot(jnp.concatenate(parts, axis=-1), wp1[...], preferred_element_type=F32)
             v = finish(acc, bias1)
             put_pairs(y1, i, v)
-        send_cols(0, a)
-        send_cols(0, h1 - 1 - a)
+        send(0, t, a, h1, e1)
         return carry
 
     lax.fori_loop(0, h1 // 2, down1, 0)
-    send_rows(0)
-
-    def wait_conv(i, a, h):
-        @pl.when(a == h // 2 - 1)
-        def _():
-            wait_cols(i, a)
-            wait_cols(i, h - 1 - a)
-
-        @pl.when(a > 0)
-        def _():
-            wait_cols(i, a - 1)
-            wait_cols(i, h - a)
-
-        @pl.when(a == 0)
-        def _():
-            wait_rows(i)
-
-    def wait_down(i, a, h):
-        hs = 2 * h
-
-        @pl.when(a == h // 2 - 1)
-        def _():
-            wait_cols(i, 2 * a + 1)
-            wait_cols(i, hs - 2 - 2 * a)
-        wait_cols(i, 2 * a)
-        wait_cols(i, hs - 1 - 2 * a)
-
-        @pl.when(a > 0)
-        def _():
-            wait_cols(i, 2 * a - 1)
-            wait_cols(i, hs - 2 * a)
-
-        @pl.when(a == 0)
-        def _():
-            wait_rows(i)
 
     bias2 = jnp.concatenate([vb2[...], vb2[...]], axis=-1)
 
     def conv1(t, carry):
-        a = h1 // 2 - 1 - t
-        wait_conv(0, a, h1)
+        a = step_of(t, h1 // 2, 3)
+        wait_conv(0, t, a, h1, 3)
         for i in (a, h1 - 1 - a):
             parts = []
             for p in range(3):
@@ -352,12 +378,10 @@
             acc = jnp.dot(jnp.concatenate(parts, axis=-1), wp2[...], preferred_element_type=F32)
             v = finish(acc, bias2)
             put_pairs(z1, i, v)
-        send_cols(1, a)
-        send_cols(1, h1 - 1 - a)
+        send(1, t, a, h1, 3)
         return carry
 
     lax.fori_loop(0, h1 // 2, conv1, 0)
-    send_rows(1)
 
     h2 = y2.shape[0] - 2
     w2 = y2.shape[1] - 2
@@ -365,8 +389,8 @@
         wcopies[i].wait()
 
     def down2(t, carry):
-        a = h2 // 2 - 1 - t
-        wait_down(1, a, h2)
+        a = step_of(t, h2 // 2, 1)
+        wait_down(1, t, a, h2, 1)
         for i in (a, h2 - 1 - a):
             parts = []
             for p in range(4):
@@ -374,18 +398,16 @@
                     parts.append(rows_of(z1, (2 * i + p, pl.ds(s // 2, w2), s % 2), w2))
             acc = jnp.dot(jnp.concatenate(parts, axis=-1), vwd2[...].reshape(16 * LANES, TILE), preferred_element_type=F32)
             y2[i + 1, pl.ds(1, w2)] = finish(acc, vb3[...]).reshape(w2, nimg, TILE)
-        send_cols(2, a)
-        send_cols(2, h2 - 1 - a)
+        send(2, t, a, h2, 1)
         return carry
 
     lax.fori_loop(0, h2 // 2, down2, 0)
-    send_rows(2)
     for i in (3, 9):
         wcopies[i].wait()
 
     def conv2(t, carry):
-        a = h2 // 2 - 1 - t
-        wait_conv(2, a, h2)
+        a = step_of(t, h2 // 2, 2)
+        wait_conv(2, t, a, h2, 2)
         for i in (a, h2 - 1 - a):
             parts = []
             for p in range(3):
@@ -395,12 +417,10 @@
             v = finish(acc, vb4[...]).reshape(w2 // 2, 2, nimg, TILE)
             z2[i + 1, pl.ds(1, w2 // 2), 0] = v[:, 0]
             z2[i + 1, pl.ds(1, w2 // 2), 1] = v[:, 1]
-        send_cols(3, a)
-        send_cols(3, h2 - 1 - a)
+        send(3, t, a, h2, 2)
         return carry
 
     lax.fori_loop(0, h2 // 2, conv2, 0)
-    send_rows(3)
 
     h3 = y3.shape[0] - 2
     w3 = y3.shape[1] - 2
@@ -413,8 +433,8 @@
             wp6[p * 3 + q, pl.ds(0, ch3), :] = vwc3[p, q]
 
     def down3(t, carry):
-        a = h3 // 2 - 1 - t
-        wait_down(3, a, h3)
+        a = step_of(t, h3 // 2, 1)
+        wait_down(3, t, a, h3, 1)
         ii = (a, h3 - 1 - a)
         acc = None
         for p in range(4):
@@ -426,16 +446,14 @@
         v = jnp.concatenate([v, jnp.zeros((v.shape[0], y3.shape[-1] - ch3), BF)], axis=-1)
         for n, i in enumerate(ii):
             y3[i + 1, pl.ds(1, w3)] = v[n * w3 * nimg:(n + 1) * w3 * nimg].reshape(w3, nimg, y3.shape[-1])
-        send_cols(4, a)
-        send_cols(4, h3 - 1 - a)
+        send(4, t, a, h3, 1)
         return carry
 
     lax.fori_loop(0, h3 // 2, down3, 0)
-    send_rows(4)
 
     def conv3(t, carry):
-        a = h3 // 2 - 1 - t
-        wait_conv(4, a, h3)
+        a = step_of(t, h3 // 2, 1)
+        wait_conv(4, t, a, h3, 1)
         ii = (a, h3 - 1 - a)
         parts = []
         for p in range(3):
@@ -495,7 +513,6 @@
         ] + [pltpu.VMEM((1, k), F32) for k in (c1, c1, c2, c2, c3, c3)] + [
             dma(d) for d in ((kk,), (12,), (2,), (2,), (kk, 2), (kk, 2), (5, 2), (5, 2), (5, 4), (5, 4), (5, hh, 2), (5, hh, 2))
         ]
-        biases = [b.reshape(1, -1) for b in (b_down1, b_conv1, b_down2, b_conv2, b_down3, b_conv3)]
         feats = pl.pallas_call(
             functools.partial(_encoder_kernel, dims),
             out_shape=jax.ShapeDtypeStruct((he, we, n, c3), BF),
@@ -503,7 +520,7 @@
             out_specs=pl.BlockSpec(memory_space=pltpu.VMEM),
             scratch_shapes=scratch,
             compiler_params=pltpu.CompilerParams(collective_id=0, has_side_effects=True, vmem_limit_bytes=62 * 1024 * 1024),
-        )(img, w_down1, biases[0], w_conv1, biases[1], w_down2, biases[2], w_conv2, biases[3], wd3, biases[4], w_conv3, biases[5])
+        )(img, w_down1, b_down1, w_conv1, b_conv1, w_down2, b_down2, w_conv2, b_conv2, wd3, b_down3, w_conv3, b_conv3)
         return jnp.transpose(feats, (2, 0, 1, 3))
 
     tile_spec = P('batch', 'row', 'col', None)

time: 69.9 us -> 66.4 us (0.950)
  local copies, waits for them, and re-layouts: 4.7 us -> 2.2 us
  Pallas kernels: 65.1 us -> 64 us
    reshape x2 -> x0, local copies, waits for them, and re-layouts: 2.5 us -> none  [local_encoder(): b.reshape(1, -1)]
    pallas_call x1, Pallas kernels: 65.1 us -> 64 us  [local_encoder(): pl.pallas_call(functools.partial(_encoder_kernel, dims), out_shape=jax.Sh...]
where the time goes in v2:
time: 66.4 us; the launch traced here: 66.2 us
  Pallas kernels  64 us (96%)
  local copies, waits for them, and re-layouts  2.2 us (3%)
    pallas_call x1, Pallas kernels, local_encoder(): pl.pallas_call(functools.partial(_encoder_kernel, dims), out_shape=jax.Sh...  64 us
    transpose x1, local copies, waits for them, and re-layouts, local_encoder(): return jnp.transpose(feats, (2, 0, 1, 3))  2.2 us

profile of v2, /device:TPU:97, one launch (start us, length us, event | category | flops | bytes accessed | tf_op | source)
XLA Modules:
  0.0 66.2 jit_solution(15002606040658851217)
XLA Ops:
  0.0 64.0 %shard_map.127 = bf16[4,16,16,320]{3,2,1,0:T(8,128)(2,1)} custom-call(bf16[16,32,64,128]{3,2,1,0:T(8,128)(2,1)} %bitcast.3, bf16[4,4,64,128]{3,2,1,0:T(8,128)(2,1)} %wd1.1, f32[128]{0:T(128)} %bd1.1, bf16[3,3,128,128]{3,2,1,0:T(8,128)(2,1)} %wc1.1, f32[128]{0:T(128)} %bc1.1, bf16[4,4,128,256]{3,2,1,0:T(8,128)(2,1)} %wd2.1, f32[256]{0:T(256)} %bd2.1, ...), custom_call_target="tpu_custom_call" | custom-call | tf_op jit(solution)/shard_map/pallas_call | solution.py:516
  64.0 2.2 %copy.14 = bf16[16,4,16,320]{3,2,1,0:T(8,128)(2,1)} copy(bf16[16,4,16,320]{3,0,2,1:T(8,128)(2,1)} %bitcast.4) | data formatting | bytes 1310720 | tf_op jit(solution)/shard_map/transpose | solution.py:524

commit v3 on v2

--- a/solution.py
+++ b/solution.py
@@ -53,12 +53,8 @@
     wcopies = [pltpu.make_async_copy(s, d, w_sem.at[i]) for i, (s, d) in enumerate(weights)]
     for i in (0, 6, 1, 7):
         wcopies[i].start()
-    for k in order:
+    for k in order[:6]:
         raw_copy(k).start()
-    first_copy.start()
-    last_copy.start()
-    for i in (2, 8, 3, 9, 4, 10, 5, 11):
-        wcopies[i].start()
 
     barrier = pltpu.get_barrier_semaphore()
     for there, dr, dc in near:
@@ -236,6 +232,16 @@
 
     def take_three(it, carry):
         ks = [middle_out(3 * it + d) for d in range(3)]
+
+        @pl.when(it < 3)
+        def _():
+            for d in range(3):
+                raw_copy(middle_out(3 * it + 6 + d)).start()
+
+        @pl.when(it == 3)
+        def _():
+            first_copy.start()
+            last_copy.start()
         sts = [st0, st1, st2]
         for k in ks:
             raw_copy(k).wait()
@@ -248,6 +254,9 @@
         return carry
 
     lax.fori_loop(0, (last - 1) // 3, take_three, 0)
+    for i in range(2, 6):
+        wcopies[i].start()
+        wcopies[i + 6].start()
 
     def take_edges():
         first_copy.wait()
@@ -276,40 +285,42 @@
         wait_cols(i, a)
         wait_cols(i, h - 1 - a)
 
-    def wait_conv(i, t, a, h, e):
+    def step_of(t, n, p):
+        up_now = (t + n - p) // n
+        return (1 - up_now) * (n - 1 - t) + up_now * (t - p)
+
+    def wait_conv(i, t, a, h, p):
         n = h // 2
-
-        @pl.when(t == (0 if e else 1))
-        def _():
-            wait_pair(i, n - 1, h)
-
-        @pl.when(jnp.logical_or(t < e, a >= 3))
-        def _():
-            wait_pair(i, a - 1, h)
-
-        @pl.when(t == e)
-        def _():
-            for s in range(min(2, n - e - 1)):
-                wait_pair(i, s, h)
+        seen = n - 1 - p if p else n
+
+        if p:
+            @pl.when(t == 0)
+            def _():
+                wait_pair(i, n - 1, h)
+
+            @pl.when(t < p)
+            def _():
+                wait_pair(i, a - 1, h)
+
+        @pl.when(t == p)
+        def _():
+            wait_pair(i, 0, h)
             wait_rows(i)
 
-    def wait_down(i, t, a, h, e):
-        n = h // 2
-
-        @pl.when(t == (0 if e else 1))
-        def _():
-            wait_pair(i, h - 1, 2 * h)
-
-        @pl.when(jnp.logical_or(t < e, a >= 2))
-        def _():
-            wait_pair(i, 2 * a, 2 * h)
-            wait_pair(i, 2 * a - 1, 2 * h)
-
-        @pl.when(t == e)
-        def _():
-            for s in range(min(3, 2 * (n - e) - 1)):
-                wait_pair(i, s, 2 * h)
+        @pl.when(jnp.logical_and(t >= p, a + 1 < seen))
+        def _():
+            wait_pair(i, a + 1, h)
+
+    def wait_down(i, a, h):
+        @pl.when(a == 0)
+        def _():
+            wait_pair(i, 0, 2 * h)
             wait_rows(i)
+        wait_pair(i, 2 * a + 1, 2 * h)
+
+        @pl.when(a < h // 2 - 1)
+        def _():
+            wait_pair(i, 2 * a + 2, 2 * h)
 
     def send(i, t, a, h, e):
         send_cols(i, a)
@@ -319,12 +330,6 @@
         def _():
             send_rows(i)
 
-    def step_of(t, n, e):
-        if not e:
-            return lax.rem(n - t, n)
-        past = (t + n - 1 - e) // n
-        return n - 1 - t + past - (n - 1 - e) * ((t + n - e) // n - past)
-
     pairs = y1.shape[1] - 2
     bias1 = jnp.concatenate([vb1[...], vb1[...]], axis=-1)
     h1 = y1.shape[0] - 2
@@ -338,20 +343,24 @@
         def _():
             wait_xcols(mid)
 
-        @pl.when(t == 1)
+        @pl.when(t == e1 - 2)
         def _():
             take_edges()
 
-        @pl.when(jnp.logical_or(t < e1, a >= 2))
+        @pl.when(t < e1)
         def _():
             wait_xcols(a)
             wait_xcols(last - a)
 
         @pl.when(t == e1)
         def _():
-            for k in (0, 1):
-                wait_xcols(k)
-                wait_xcols(last - k)
+            wait_xcols(0)
+            wait_xcols(last)
+
+        @pl.when(jnp.logical_and(t >= e1, a + 1 < h1 // 2 - e1))
+        def _():
+            wait_xcols(a + 1)
+            wait_xcols(last - 1 - a)
         for i in (a, h1 - 1 - a):
             parts = []
             for dk in range(2):
@@ -368,8 +377,8 @@
     bias2 = jnp.concatenate([vb2[...], vb2[...]], axis=-1)
 
     def conv1(t, carry):
-        a = step_of(t, h1 // 2, 3)
-        wait_conv(0, t, a, h1, 3)
+        a = step_of(t, h1 // 2, 2)
+        wait_conv(0, t, a, h1, 2)
         for i in (a, h1 - 1 - a):
             parts = []
             for p in range(3):
@@ -378,19 +387,20 @@
             acc = jnp.dot(jnp.concatenate(parts, axis=-1), wp2[...], preferred_element_type=F32)
             v = finish(acc, bias2)
             put_pairs(z1, i, v)
-        send(1, t, a, h1, 3)
+        send(1, t, a, h1, 2)
         return carry
 
     lax.fori_loop(0, h1 // 2, conv1, 0)
 
+    ch3 = out.shape[-1]
     h2 = y2.shape[0] - 2
     w2 = y2.shape[1] - 2
     for i in (2, 8):
         wcopies[i].wait()
 
     def down2(t, carry):
-        a = step_of(t, h2 // 2, 1)
-        wait_down(1, t, a, h2, 1)
+        a = t
+        wait_down(1, a, h2)
         for i in (a, h2 - 1 - a):
             parts = []
             for p in range(4):
@@ -398,16 +408,20 @@
                     parts.append(rows_of(z1, (2 * i + p, pl.ds(s // 2, w2), s % 2), w2))
             acc = jnp.dot(jnp.concatenate(parts, axis=-1), vwd2[...].reshape(16 * LANES, TILE), preferred_element_type=F32)
             y2[i + 1, pl.ds(1, w2)] = finish(acc, vb3[...]).reshape(w2, nimg, TILE)
-        send(2, t, a, h2, 1)
+        send(2, t, a, h2, 0)
         return carry
 
     lax.fori_loop(0, h2 // 2, down2, 0)
-    for i in (3, 9):
+    for i in (3, 9, 5):
         wcopies[i].wait()
+    wp6[...] = jnp.zeros(wp6.shape, BF)
+    for p in range(3):
+        for q in range(3):
+            wp6[p * 3 + q, pl.ds(0, ch3), :] = vwc3[p, q]
 
     def conv2(t, carry):
-        a = step_of(t, h2 // 2, 2)
-        wait_conv(2, t, a, h2, 2)
+        a = t
+        wait_conv(2, t, a, h2, 0)
         for i in (a, h2 - 1 - a):
             parts = []
             for p in range(3):
@@ -417,24 +431,19 @@
             v = finish(acc, vb4[...]).reshape(w2 // 2, 2, nimg, TILE)
             z2[i + 1, pl.ds(1, w2 // 2), 0] = v[:, 0]
             z2[i + 1, pl.ds(1, w2 // 2), 1] = v[:, 1]
-        send(3, t, a, h2, 2)
+        send(3, t, a, h2, 0)
         return carry
 
     lax.fori_loop(0, h2 // 2, conv2, 0)
 
     h3 = y3.shape[0] - 2
     w3 = y3.shape[1] - 2
-    ch3 = out.shape[-1]
-    for i in (4, 10, 5, 11):
+    for i in (4, 10, 11):
         wcopies[i].wait()
-    wp6[...] = jnp.zeros(wp6.shape, BF)
-    for p in range(3):
-        for q in range(3):
-            wp6[p * 3 + q, pl.ds(0, ch3), :] = vwc3[p, q]
 
     def down3(t, carry):
-        a = step_of(t, h3 // 2, 1)
-        wait_down(3, t, a, h3, 1)
+        a = t
+        wait_down(3, a, h3)
         ii = (a, h3 - 1 - a)
         acc = None
         for p in range(4):
@@ -446,26 +455,31 @@
         v = jnp.concatenate([v, jnp.zeros((v.shape[0], y3.shape[-1] - ch3), BF)], axis=-1)
         for n, i in enumerate(ii):
             y3[i + 1, pl.ds(1, w3)] = v[n * w3 * nimg:(n + 1) * w3 * nimg].reshape(w3, nimg, y3.shape[-1])
-        send(4, t, a, h3, 1)
+        send(4, t, a, h3, 0)
         return carry
 
     lax.fori_loop(0, h3 // 2, down3, 0)
 
-    def conv3(t, carry):
-        a = step_of(t, h3 // 2, 1)
-        wait_conv(4, t, a, h3, 1)
-        ii = (a, h3 - 1 - a)
+    inner = [(i, 1, w3 - 2) for i in range(1, h3 - 1)]
+    border = [(0, 0, w3), (h3 - 1, 0, w3)] + [(i, c, 1) for i in range(1, h3 - 1) for c in (0, w3 - 1)]
+
+    def conv3(strips):
         parts = []
         for p in range(3):
             for q in range(3):
-                parts.append(jnp.concatenate([rows_of(y3, (i + p, pl.ds(q, w3)), w3) for i in ii], axis=0))
+                parts.append(jnp.concatenate([rows_of(y3, (i + p, pl.ds(c + q, w)), w) for i, c, w in strips], axis=0))
         acc = jnp.dot(jnp.concatenate(parts, axis=-1), wp6[...].reshape(9 * wp6.shape[1], ch3), preferred_element_type=F32)
         v = finish(acc, vb6[...])
-        for n, i in enumerate(ii):
-            out[i] = v[n * w3 * nimg:(n + 1) * w3 * nimg].reshape(w3, nimg, ch3)
-        return carry
-
-    lax.fori_loop(0, h3 // 2, conv3, 0)
+        at = 0
+        for i, c, w in strips:
+            out[i, pl.ds(c, w)] = v[at:at + w * nimg].reshape(w, nimg, ch3)
+            at += w * nimg
+
+    conv3(inner)
+    for r in range(h3):
+        wait_cols(4, r)
+    wait_rows(4)
+    conv3(border)
 
     each(ends, lambda s: raw_send(s).wait_send())
 

time: 66.4 us -> 61.5 us (0.926)
  Pallas kernels: 64 us -> 59.1 us
    pallas_call x1, Pallas kernels: 64 us -> 59.1 us  [local_encoder(): pl.pallas_call(functools.partial(_encoder_kernel, dims), out_shape=jax.Sh...]
where the time goes in v3:
time: 61.5 us; the launch traced here: 61.3 us
  Pallas kernels  59.1 us (96%)
  local copies, waits for them, and re-layouts  2.2 us (4%)
    pallas_call x1, Pallas kernels, local_encoder(): pl.pallas_call(functools.partial(_encoder_kernel, dims), out_shape=jax.Sh...  59.1 us
    transpose x1, local copies, waits for them, and re-layouts, local_encoder(): return jnp.transpose(feats, (2, 0, 1, 3))  2.2 us

profile of v3, /device:TPU:97, one launch (start us, length us, event | category | flops | bytes accessed | tf_op | source)
XLA Modules:
  0.0 61.3 jit_solution(7950336803843775872)
XLA Ops:
  0.0 59.1 %shard_map.127 = bf16[4,16,16,320]{3,2,1,0:T(8,128)(2,1)} custom-call(bf16[16,32,64,128]{3,2,1,0:T(8,128)(2,1)} %bitcast.3, bf16[4,4,64,128]{3,2,1,0:T(8,128)(2,1)} %wd1.1, f32[128]{0:T(128)} %bd1.1, bf16[3,3,128,128]{3,2,1,0:T(8,128)(2,1)} %wc1.1, f32[128]{0:T(128)} %bc1.1, bf16[4,4,128,256]{3,2,1,0:T(8,128)(2,1)} %wd2.1, f32[256]{0:T(256)} %bd2.1, ...), custom_call_target="tpu_custom_call" | custom-call | tf_op jit(solution)/shard_map/pallas_call | solution.py:530
  59.1 2.2 %copy.14 = bf16[16,4,16,320]{3,2,1,0:T(8,128)(2,1)} copy(bf16[16,4,16,320]{3,0,2,1:T(8,128)(2,1)} %bitcast.4) | data formatting | bytes 1310720 | tf_op jit(solution)/shard_map/transpose | solution.py:538

commit v4 on v3

--- a/solution.py
+++ b/solution.py
@@ -153,7 +153,7 @@
         b = bufs[i]
         ref = b['ref']
         src, dst, dc = (b['first'], b['hr'], -1) if s == 0 else (b['last'], b['hl'], 1)
-        return pltpu.make_async_remote_copy(ref.at[(r + 1,) + src], ref.at[(r + 1,) + dst], col_send.at[i, r, s], col_recv.at[i, r, s],
+        return pltpu.make_async_remote_copy(ref.at[(r + 1,) + src], ref.at[(r + 1,) + dst], col_send.at[i, s], col_recv.at[i, r, s],
                                             device_id=dev(0, dc), device_id_type=pl.DeviceIdType.MESH)
 
     sides = ((left, 0), (right, 1))
@@ -186,7 +186,7 @@
 
     def xcol_copy(k, s):
         src, dst, dc = ((1, 0), (xu + 1, 0), -1) if s == 0 else ((xu, 3), (0, 3), 1)
-        return pltpu.make_async_remote_copy(xt.at[(k,) + src], xt.at[(k,) + dst], xc_send.at[k, s], xc_recv.at[k, s],
+        return pltpu.make_async_remote_copy(xt.at[(k,) + src], xt.at[(k,) + dst], xc_send.at[s], xc_recv.at[k, s],
                                             device_id=dev(0, dc), device_id_type=pl.DeviceIdType.MESH)
 
     def send_xcols(k):
@@ -307,7 +307,7 @@
             wait_pair(i, 0, h)
             wait_rows(i)
 
-        @pl.when(jnp.logical_and(t >= p, a + 1 < seen))
+        @pl.when((t >= p) & (a + 1 < seen))
         def _():
             wait_pair(i, a + 1, h)
 
@@ -336,16 +336,10 @@
 
     e1 = 4
 
-    def down1(t, carry):
-        a = step_of(t, h1 // 2, e1)
-
+    def wait_images(t, a):
         @pl.when(t == 0)
         def _():
             wait_xcols(mid)
-
-        @pl.when(t == e1 - 2)
-        def _():
-            take_edges()
 
         @pl.when(t < e1)
         def _():
@@ -357,10 +351,12 @@
             wait_xcols(0)
             wait_xcols(last)
 
-        @pl.when(jnp.logical_and(t >= e1, a + 1 < h1 // 2 - e1))
+        @pl.when((t >= e1) & (a + 1 < h1 // 2 - e1))
         def _():
             wait_xcols(a + 1)
             wait_xcols(last - 1 - a)
+
+    def down1(a):
         for i in (a, h1 - 1 - a):
             parts = []
             for dk in range(2):
@@ -369,16 +365,40 @@
             acc = jnp.dot(jnp.concatenate(parts, axis=-1), wp1[...], preferred_element_type=F32)
             v = finish(acc, bias1)
             put_pairs(y1, i, v)
-        send(0, t, a, h1, e1)
-        return carry
-
-    lax.fori_loop(0, h1 // 2, down1, 0)
+
+    def two_steps(wait, step, i, h, p, before=lambda t2: None):
+        def body(t2, carry):
+            before(t2)
+            ts = [2 * t2, 2 * t2 + 1]
+            steps = [step_of(t, h // 2, p) for t in ts]
+            for t, a in zip(ts, steps):
+                wait(t, a)
+            for a in steps:
+                step(a)
+            for t, a in zip(ts, steps):
+                send(i, t, a, h, p)
+            return carry
+        lax.fori_loop(0, h // 4, body, 0)
+
+    def first_then_rest(wait, step, i, h):
+        for steps in ([0], list(range(1, h // 2))):
+            for a in steps:
+                wait(a, a)
+            for a in steps:
+                step(a)
+            for a in steps:
+                send(i, a, a, h, 0)
+
+    def edges_at(t2):
+        @pl.when(t2 == e1 // 2 - 1)
+        def _():
+            take_edges()
+
+    two_steps(wait_images, down1, 0, h1, e1, edges_at)
 
     bias2 = jnp.concatenate([vb2[...], vb2[...]], axis=-1)
 
-    def conv1(t, carry):
-        a = step_of(t, h1 // 2, 2)
-        wait_conv(0, t, a, h1, 2)
+    def conv1(a):
         for i in (a, h1 - 1 - a):
             parts = []
             for p in range(3):
@@ -387,10 +407,8 @@
             acc = jnp.dot(jnp.concatenate(parts, axis=-1), wp2[...], preferred_element_type=F32)
             v = finish(acc, bias2)
             put_pairs(z1, i, v)
-        send(1, t, a, h1, 2)
-        return carry
-
-    lax.fori_loop(0, h1 // 2, conv1, 0)
+
+    two_steps(lambda t, a: wait_conv(0, t, a, h1, 2), conv1, 1, h1, 2)
 
     ch3 = out.shape[-1]
     h2 = y2.shape[0] - 2
@@ -398,9 +416,7 @@
     for i in (2, 8):
         wcopies[i].wait()
 
-    def down2(t, carry):
-        a = t
-        wait_down(1, a, h2)
+    def down2(a):
         for i in (a, h2 - 1 - a):
             parts = []
             for p in range(4):
@@ -408,10 +424,8 @@
                     parts.append(rows_of(z1, (2 * i + p, pl.ds(s // 2, w2), s % 2), w2))
             acc = jnp.dot(jnp.concatenate(parts, axis=-1), vwd2[...].reshape(16 * LANES, TILE), preferred_element_type=F32)
             y2[i + 1, pl.ds(1, w2)] = finish(acc, vb3[...]).reshape(w2, nimg, TILE)
-        send(2, t, a, h2, 0)
-        return carry
-
-    lax.fori_loop(0, h2 // 2, down2, 0)
+
+    first_then_rest(lambda t, a: wait_down(1, a, h2), down2, 2, h2)
     for i in (3, 9, 5):
         wcopies[i].wait()
     wp6[...] = jnp.zeros(wp6.shape, BF)
@@ -419,9 +433,7 @@
         for q in range(3):
             wp6[p * 3 + q, pl.ds(0, ch3), :] = vwc3[p, q]
 
-    def conv2(t, carry):
-        a = t
-        wait_conv(2, t, a, h2, 0)
+    def conv2(a):
         for i in (a, h2 - 1 - a):
             parts = []
             for p in range(3):
@@ -431,10 +443,8 @@
             v = finish(acc, vb4[...]).reshape(w2 // 2, 2, nimg, TILE)
             z2[i + 1, pl.ds(1, w2 // 2), 0] = v[:, 0]
             z2[i + 1, pl.ds(1, w2 // 2), 1] = v[:, 1]
-        send(3, t, a, h2, 0)
-        return carry
-
-    lax.fori_loop(0, h2 // 2, conv2, 0)
+
+    first_then_rest(lambda t, a: wait_conv(2, t, a, h2, 0), conv2, 3, h2)
 
     h3 = y3.shape[0] - 2
     w3 = y3.shape[1] - 2
@@ -483,17 +493,15 @@
 
     each(ends, lambda s: raw_send(s).wait_send())
 
-    def drain(make, count):
-        def one(r, carry):
-            make(r).wait_send()
-            return carry
-        lax.fori_loop(0, count, one, 0)
-
-    each(sides, lambda s: drain(lambda k: xcol_copy(k, s), last + 1))
+    def drain_cols(ref, rows, at, sem):
+        whole = ref.at[(rows,) + at]
+        pltpu.make_async_remote_copy(whole, whole, sem, sem, device_id=dev(0, 0), device_id_type=pl.DeviceIdType.MESH).wait_send()
+
+    each(sides, lambda s: drain_cols(xt, pl.ds(0, last + 1), (1, 0), xc_send.at[s]))
     for i, b in enumerate(bufs):
         each(ends, lambda s: row_copy(i, s).wait_send())
         each(corners, lambda s: corner_copy(i, s).wait_send())
-        each(sides, lambda s: drain(lambda r: col_copy(i, r, s), b['h']))
+        each(sides, lambda s: drain_cols(b['ref'], pl.ds(1, b['h']), b['first'], col_send.at[i, s]))
 
 
 def solution(mesh):
@@ -525,7 +533,7 @@
             pltpu.VMEM((6 * TILE, TILE), BF),
             pltpu.VMEM((9, c3p, c3), BF),
         ] + [pltpu.VMEM((1, k), F32) for k in (c1, c1, c2, c2, c3, c3)] + [
-            dma(d) for d in ((kk,), (12,), (2,), (2,), (kk, 2), (kk, 2), (5, 2), (5, 2), (5, 4), (5, 4), (5, hh, 2), (5, hh, 2))
+            dma(d) for d in ((kk,), (12,), (2,), (2,), (2,), (kk, 2), (5, 2), (5, 2), (5, 4), (5, 4), (5, 2), (5, hh, 2))
         ]
         feats = pl.pallas_call(
             functools.partial(_encoder_kernel, dims),

time: 61.5 us -> 62.4 us (1.015)
  Pallas kernels: 59.1 us -> 60.1 us
    pallas_call x1, Pallas kernels: 59.1 us -> 60.1 us  [local_encoder(): pl.pallas_call(functools.partial(_encoder_kernel, dims), out_shape=jax.Sh...]
where the time goes in v4:
time: 62.4 us; the launch traced here: 62.3 us
  Pallas kernels  60.1 us (96%)
  local copies, waits for them, and re-layouts  2.2 us (4%)
    pallas_call x1, Pallas kernels, local_encoder(): pl.pallas_call(functools.partial(_encoder_kernel, dims), out_shape=jax.Sh...  60.1 us
    transpose x1, local copies, waits for them, and re-layouts, local_encoder(): return jnp.transpose(feats, (2, 0, 1, 3))  2.2 us

profile of v4, /device:TPU:97, one launch (start us, length us, event | category | flops | bytes accessed | tf_op | source)
XLA Modules:
  0.0 62.3 jit_solution(12321769754482934206)
XLA Ops:
  0.0 60.1 %shard_map.127 = bf16[4,16,16,320]{3,2,1,0:T(8,128)(2,1)} custom-call(bf16[16,32,64,128]{3,2,1,0:T(8,128)(2,1)} %bitcast.3, bf16[4,4,64,128]{3,2,1,0:T(8,128)(2,1)} %wd1.1, f32[128]{0:T(128)} %bd1.1, bf16[3,3,128,128]{3,2,1,0:T(8,128)(2,1)} %wc1.1, f32[128]{0:T(128)} %bc1.1, bf16[4,4,128,256]{3,2,1,0:T(8,128)(2,1)} %wd2.1, f32[256]{0:T(256)} %bd2.1, ...), custom_call_target="tpu_custom_call" | custom-call | tf_op jit(solution)/shard_map/pallas_call | solution.py:538
  60.1 2.2 %copy.14 = bf16[16,4,16,320]{3,2,1,0:T(8,128)(2,1)} copy(bf16[16,4,16,320]{3,0,2,1:T(8,128)(2,1)} %bitcast.4) | data formatting | bytes 1310720 | tf_op jit(solution)/shard_map/transpose | solution.py:546

commit v5 on v3

--- a/solution.py
+++ b/solution.py
@@ -153,7 +153,7 @@
         b = bufs[i]
         ref = b['ref']
         src, dst, dc = (b['first'], b['hr'], -1) if s == 0 else (b['last'], b['hl'], 1)
-        return pltpu.make_async_remote_copy(ref.at[(r + 1,) + src], ref.at[(r + 1,) + dst], col_send.at[i, r, s], col_recv.at[i, r, s],
+        return pltpu.make_async_remote_copy(ref.at[(r + 1,) + src], ref.at[(r + 1,) + dst], col_send.at[i, s], col_recv.at[i, r, s],
                                             device_id=dev(0, dc), device_id_type=pl.DeviceIdType.MESH)
 
     sides = ((left, 0), (right, 1))
@@ -165,12 +165,6 @@
             def _(s=s):
                 act(s)
 
-    def send_cols(i, r):
-        each(sides, lambda s: col_copy(i, r, s).start())
-
-    def wait_cols(i, r):
-        each(from_sides, lambda s: col_copy(i, r, s).wait_recv())
-
     ends = list(zip((up, down), range(2)))
     from_ends = list(zip((down, up), range(2)))
     corners = [(x[0], s) for s, x in enumerate(near[4:])]
@@ -186,32 +180,42 @@
 
     def xcol_copy(k, s):
         src, dst, dc = ((1, 0), (xu + 1, 0), -1) if s == 0 else ((xu, 3), (0, 3), 1)
-        return pltpu.make_async_remote_copy(xt.at[(k,) + src], xt.at[(k,) + dst], xc_send.at[k, s], xc_recv.at[k, s],
+        return pltpu.make_async_remote_copy(xt.at[(k,) + src], xt.at[(k,) + dst], xc_send.at[s], xc_recv.at[k, s],
                                             device_id=dev(0, dc), device_id_type=pl.DeviceIdType.MESH)
 
-    def send_xcols(k):
-        each(sides, lambda s: xcol_copy(k, s).start())
-
-    def wait_xcols(k):
-        each(from_sides, lambda s: xcol_copy(k, s).wait_recv())
+    def send_xcols(ks):
+        each(sides, lambda s: [xcol_copy(k, s).start() for k in ks])
+
+    def wait_xcols(*ks):
+        each(from_sides, lambda s: [xcol_copy(k, s).wait_recv() for k in ks])
 
     for i in (0, 1, 6, 7):
         wcopies[i].wait()
-    zb = jnp.zeros((64, LANES), BF)
-    for dk in range(2):
-        for dc in range(3):
-            for cpar in range(2):
-                for rpar in range(2):
-                    r0 = (dk * 3 + dc) * TILE + (cpar * 2 + rpar) * 64
-                    for j in range(2):
-                        q = 2 * (dc - j) + cpar
-                        wp1[pl.ds(r0, 64), pl.ds(j * LANES, LANES)] = vwd1[2 * dk + rpar, q] if 0 <= q < 4 else zb
-    zc = jnp.zeros((LANES, LANES), BF)
-    for p in range(3):
-        for s in range(4):
-            for j in range(2):
-                q = s - j
-                wp2[pl.ds((p * 4 + s) * LANES, LANES), pl.ds(j * LANES, LANES)] = vwc1[p, q] if 0 <= q < 3 else zc
+
+    def loop(count, act):
+        def body(i, carry):
+            act(i)
+            return carry
+        lax.fori_loop(0, count, body, 0)
+
+    def zero_block(ref):
+        def act(i):
+            zero(ref.at[i])
+        return act
+
+    def fill1(i):
+        dk, dc, cpar, rpar = i // 8, i // 4 % 2, i // 2 % 2, i % 2
+        for j in range(2):
+            wp1[(dk * 3 + dc + j) * 4 + cpar * 2 + rpar, :, pl.ds(j * LANES, LANES)] = vwd1[2 * dk + rpar, 2 * dc + cpar]
+
+    def fill2(i):
+        for j in range(2):
+            wp2[i // 3 * 4 + i % 3 + j, :, pl.ds(j * LANES, LANES)] = vwc1[i // 3, i % 3]
+
+    loop(wp1.shape[0], zero_block(wp1))
+    loop(wp2.shape[0], zero_block(wp2))
+    loop(16, fill1)
+    loop(9, fill2)
 
     eye = (lax.broadcasted_iota(jnp.int32, (LANES, LANES), 0) == lax.broadcasted_iota(jnp.int32, (LANES, LANES), 1)).astype(F32).astype(BF)
 
@@ -230,45 +234,42 @@
         h = (t + 1) // 2
         return mid + h * (1 - 2 * (t % 2))
 
+    inner = (last - 1) // 3
+
     def take_three(it, carry):
-        ks = [middle_out(3 * it + d) for d in range(3)]
-
-        @pl.when(it < 3)
+        edge = it // inner
+        ks = [edge * (last * min(d, 1)) + (1 - edge) * middle_out(3 * it + d) for d in range(3)]
+
+        @pl.when(it < inner - 2)
         def _():
             for d in range(3):
                 raw_copy(middle_out(3 * it + 6 + d)).start()
 
-        @pl.when(it == 3)
+        @pl.when(it == inner - 2)
         def _():
             first_copy.start()
             last_copy.start()
-        sts = [st0, st1, st2]
-        for k in ks:
-            raw_copy(k).wait()
-        for k, st in zip(ks, sts):
+
+        @pl.when(it < inner)
+        def _():
+            for k in ks:
+                raw_copy(k).wait()
+
+        @pl.when(it == inner)
+        def _():
+            first_copy.wait()
+            last_copy.wait()
+            each(from_ends, lambda s: raw_send(s).wait_recv())
+        for k, st in zip(ks, (st0, st1, st2)):
             transpose_in(k, st)
-        for k, st in zip(ks, sts):
+        for k, st in zip(ks, (st0, st1, st2)):
             transpose_out(k, st)
-        for k in ks:
-            send_xcols(k)
-        return carry
-
-    lax.fori_loop(0, (last - 1) // 3, take_three, 0)
-    for i in range(2, 6):
-        wcopies[i].start()
-        wcopies[i + 6].start()
-
-    def take_edges():
-        first_copy.wait()
-        last_copy.wait()
-
-        each(from_ends, lambda s: raw_send(s).wait_recv())
-        transpose_in(0, st0)
-        transpose_in(last, st1)
-        transpose_out(0, st0)
-        transpose_out(last, st1)
-        send_xcols(0)
-        send_xcols(last)
+        send_xcols(ks[:2])
+
+        @pl.when(it < inner)
+        def _():
+            send_xcols(ks[2:])
+        return carry
 
     def finish(acc, bias):
         return jnp.maximum(acc + bias, 0.0).astype(BF)
@@ -282,8 +283,7 @@
         return v.reshape(w * nimg, v.shape[-1])
 
     def wait_pair(i, a, h):
-        wait_cols(i, a)
-        wait_cols(i, h - 1 - a)
+        each(from_sides, lambda s: [col_copy(i, r, s).wait_recv() for r in (a, h - 1 - a)])
 
     def step_of(t, n, p):
         up_now = (t + n - p) // n
@@ -323,8 +323,7 @@
             wait_pair(i, 2 * a + 2, 2 * h)
 
     def send(i, t, a, h, e):
-        send_cols(i, a)
-        send_cols(i, h - 1 - a)
+        each(sides, lambda s: [col_copy(i, r, s).start() for r in (a, h - 1 - a)])
 
         @pl.when(t == e)
         def _():
@@ -343,36 +342,40 @@
         def _():
             wait_xcols(mid)
 
-        @pl.when(t == e1 - 2)
-        def _():
-            take_edges()
-
         @pl.when(t < e1)
         def _():
-            wait_xcols(a)
-            wait_xcols(last - a)
+            wait_xcols(a, last - a)
 
         @pl.when(t == e1)
         def _():
-            wait_xcols(0)
-            wait_xcols(last)
+            wait_xcols(0, last)
 
         @pl.when(jnp.logical_and(t >= e1, a + 1 < h1 // 2 - e1))
         def _():
-            wait_xcols(a + 1)
-            wait_xcols(last - 1 - a)
+            wait_xcols(a + 1, last - 1 - a)
         for i in (a, h1 - 1 - a):
             parts = []
             for dk in range(2):
                 for p in range(3, 9):
                     parts.append(rows_of(xt, (i + dk, pl.ds(p // 4, pairs), p % 4), pairs))
-            acc = jnp.dot(jnp.concatenate(parts, axis=-1), wp1[...], preferred_element_type=F32)
+            acc = jnp.dot(jnp.concatenate(parts, axis=-1), wp1[...].reshape(6 * TILE, TILE), preferred_element_type=F32)
             v = finish(acc, bias1)
             put_pairs(y1, i, v)
         send(0, t, a, h1, e1)
         return carry
 
-    lax.fori_loop(0, h1 // 2, down1, 0)
+    def phase(ph, carry):
+        lax.fori_loop(inner * ph, inner + ph, take_three, 0)
+
+        @pl.when(ph == 0)
+        def _():
+            for i in range(2, 6):
+                wcopies[i].start()
+                wcopies[i + 6].start()
+        lax.fori_loop((e1 - 2) * ph, e1 - 2 + (h1 // 2 - e1 + 2) * ph, down1, 0)
+        return carry
+
+    lax.fori_loop(0, 2, phase, 0)
 
     bias2 = jnp.concatenate([vb2[...], vb2[...]], axis=-1)
 
@@ -384,7 +387,7 @@
             for p in range(3):
                 for s in range(1, 5):
                     parts.append(rows_of(y1, (i + p, pl.ds(s // 2, pairs), s % 2), pairs))
-            acc = jnp.dot(jnp.concatenate(parts, axis=-1), wp2[...], preferred_element_type=F32)
+            acc = jnp.dot(jnp.concatenate(parts, axis=-1), wp2[...].reshape(6 * TILE, TILE), preferred_element_type=F32)
             v = finish(acc, bias2)
             put_pairs(z1, i, v)
         send(1, t, a, h1, 2)
@@ -414,10 +417,12 @@
     lax.fori_loop(0, h2 // 2, down2, 0)
     for i in (3, 9, 5):
         wcopies[i].wait()
-    wp6[...] = jnp.zeros(wp6.shape, BF)
-    for p in range(3):
-        for q in range(3):
-            wp6[p * 3 + q, pl.ds(0, ch3), :] = vwc3[p, q]
+
+    def fill6(i):
+        wp6[i, pl.ds(0, ch3), :] = vwc3[i // 3, i % 3]
+        wp6[i, pl.ds(ch3, wp6.shape[1] - ch3), :] = jnp.zeros((wp6.shape[1] - ch3, ch3), BF)
+
+    loop(9, fill6)
 
     def conv2(t, carry):
         a = t
@@ -445,12 +450,12 @@
         a = t
         wait_down(3, a, h3)
         ii = (a, h3 - 1 - a)
-        acc = None
+        parts, wts = [], []
         for p in range(4):
             for s in range(1, 5):
-                lhs = jnp.concatenate([rows_of(z2, (2 * i + p, pl.ds(s // 2, w3), s % 2), w3) for i in ii], axis=0)
-                d = lax.dot_general(lhs, vwd3[p, s - 1], BY_LAST, preferred_element_type=F32)
-                acc = d if acc is None else acc + d
+                parts.append(jnp.concatenate([rows_of(z2, (2 * i + p, pl.ds(s // 2, w3), s % 2), w3) for i in ii], axis=0))
+                wts.append(vwd3[p, s - 1])
+        acc = lax.dot_general(jnp.concatenate(parts, axis=-1), jnp.concatenate(wts, axis=-1), BY_LAST, preferred_element_type=F32)
         v = finish(acc, vb5[...])
         v = jnp.concatenate([v, jnp.zeros((v.shape[0], y3.shape[-1] - ch3), BF)], axis=-1)
         for n, i in enumerate(ii):
@@ -460,10 +465,14 @@
 
     lax.fori_loop(0, h3 // 2, down3, 0)
 
-    inner = [(i, 1, w3 - 2) for i in range(1, h3 - 1)]
-    border = [(0, 0, w3), (h3 - 1, 0, w3)] + [(i, c, 1) for i in range(1, h3 - 1) for c in (0, w3 - 1)]
-
-    def conv3(strips):
+    def conv3(t, carry):
+        @pl.when(t == 1)
+        def _():
+            for r in range(h3 // 2):
+                wait_pair(4, r, h3)
+            wait_rows(4)
+        top, bottom, lo, hi = 1 - t, h3 - 2 + t, 1 - t, w3 - 2 + t
+        strips = [(i, 1, w3 - 2) for i in (top, bottom)] + [(i, c, 1) for i in (top, bottom, *range(1, h3 - 1)) for c in (lo, hi)]
         parts = []
         for p in range(3):
             for q in range(3):
@@ -474,26 +483,21 @@
         for i, c, w in strips:
             out[i, pl.ds(c, w)] = v[at:at + w * nimg].reshape(w, nimg, ch3)
             at += w * nimg
-
-    conv3(inner)
-    for r in range(h3):
-        wait_cols(4, r)
-    wait_rows(4)
-    conv3(border)
+        return carry
+
+    lax.fori_loop(0, 2, conv3, 0)
 
     each(ends, lambda s: raw_send(s).wait_send())
 
-    def drain(make, count):
-        def one(r, carry):
-            make(r).wait_send()
-            return carry
-        lax.fori_loop(0, count, one, 0)
-
-    each(sides, lambda s: drain(lambda k: xcol_copy(k, s), last + 1))
+    def drain_cols(ref, rows, at, sem):
+        whole = ref.at[(rows,) + at]
+        pltpu.make_async_remote_copy(whole, whole, sem, sem, device_id=dev(0, 0), device_id_type=pl.DeviceIdType.MESH).wait_send()
+
+    each(sides, lambda s: drain_cols(xt, pl.ds(0, last + 1), (1, 0), xc_send.at[s]))
     for i, b in enumerate(bufs):
         each(ends, lambda s: row_copy(i, s).wait_send())
         each(corners, lambda s: corner_copy(i, s).wait_send())
-        each(sides, lambda s: drain(lambda r: col_copy(i, r, s), b['h']))
+        each(sides, lambda s: drain_cols(b['ref'], pl.ds(1, b['h']), b['first'], col_send.at[i, s]))
 
 
 def solution(mesh):
@@ -521,11 +525,11 @@
         ] + [pltpu.VMEM((n * PITCH, LANES), F32)] * 3 + [
             pltpu.VMEM(x.shape, BF) for x in (w_down1, w_conv1, w_down2, w_conv2, wd3, w_conv3)
         ] + [
-            pltpu.VMEM((6 * TILE, TILE), BF),
-            pltpu.VMEM((6 * TILE, TILE), BF),
+            pltpu.VMEM((24, c, TILE), BF),
+            pltpu.VMEM((12, c1, TILE), BF),
             pltpu.VMEM((9, c3p, c3), BF),
         ] + [pltpu.VMEM((1, k), F32) for k in (c1, c1, c2, c2, c3, c3)] + [
-            dma(d) for d in ((kk,), (12,), (2,), (2,), (kk, 2), (kk, 2), (5, 2), (5, 2), (5, 4), (5, 4), (5, hh, 2), (5, hh, 2))
+            dma(d) for d in ((kk,), (12,), (2,), (2,), (2,), (kk, 2), (5, 2), (5, 2), (5, 4), (5, 4), (5, 2), (5, hh, 2))
         ]
         feats = pl.pallas_call(
             functools.partial(_encoder_kernel, dims),

time: 61.5 us -> 60.2 us (0.979)
  Pallas kernels: 59.1 us -> 57.8 us
    pallas_call x1, Pallas kernels: 59.1 us -> 57.8 us  [local_encoder(): pl.pallas_call(functools.partial(_encoder_kernel, dims), out_shape=jax.Sh...]
where the time goes in v5:
time: 60.2 us; the launch traced here: 60 us
  Pallas kernels  57.8 us (96%)
  local copies, waits for them, and re-layouts  2.2 us (4%)
    pallas_call x1, Pallas kernels, local_encoder(): pl.pallas_call(functools.partial(_encoder_kernel, dims), out_shape=jax.Sh...  57.8 us
    transpose x1, local copies, waits for them, and re-layouts, local_encoder(): return jnp.transpose(feats, (2, 0, 1, 3))  2.2 us

profile of v5, /device:TPU:97, one launch (start us, length us, event | category | flops | bytes accessed | tf_op | source)
XLA Modules:
  0.0 60.0 jit_solution(4115572031247051784)
XLA Ops:
  0.0 57.8 %shard_map.127 = bf16[4,16,16,320]{3,2,1,0:T(8,128)(2,1)} custom-call(bf16[16,32,64,128]{3,2,1,0:T(8,128)(2,1)} %bitcast.3, bf16[4,4,64,128]{3,2,1,0:T(8,128)(2,1)} %wd1.1, f32[128]{0:T(128)} %bd1.1, bf16[3,3,128,128]{3,2,1,0:T(8,128)(2,1)} %wc1.1, f32[128]{0:T(128)} %bc1.1, bf16[4,4,128,256]{3,2,1,0:T(8,128)(2,1)} %wd2.1, f32[256]{0:T(256)} %bd2.1, ...), custom_call_target="tpu_custom_call" | custom-call | tf_op jit(solution)/shard_map/pallas_call | solution.py:534
  57.8 2.2 %copy.14 = bf16[16,4,16,320]{3,2,1,0:T(8,128)(2,1)} copy(bf16[16,4,16,320]{3,0,2,1:T(8,128)(2,1)} %bitcast.4) | data formatting | bytes 1310720 | tf_op jit(solution)/shard_map/transpose | solution.py:542

commit v6 on v5

--- a/solution.py
+++ b/solution.py
@@ -79,16 +79,19 @@
     def zero(ref):
         ref[...] = jnp.zeros(ref.shape, ref.dtype)
 
-    def wide(ref, h):
-        u = ref.shape[1] - 2
-        return dict(ref=ref, h=h, hl=(0, 1), first=(1, 0), last=(u, 1), hr=(u + 1, 0), real=pl.ds(1, u))
-
-    def flat(ref, h):
-        w = ref.shape[1] - 2
-        return dict(ref=ref, h=h, hl=(0,), first=(1,), last=(w,), hr=(w + 1,), real=pl.ds(1, w))
-
-    bufs = [wide(y1, y1.shape[0] - 2), wide(z1, z1.shape[0] - 2), flat(y2, y2.shape[0] - 2), wide(z2, z2.shape[0] - 2),
-            flat(y3, y3.shape[0] - 2)]
+    def buf(ref, cut):
+        h, u = ref.shape[0] - 2, ref.shape[1] - 2
+        if len(ref.shape) > 4:
+            where = dict(hl=(0, 1), first=(1, 0), last=(u, 1), hr=(u + 1, 0))
+        else:
+            where = dict(hl=(0,), first=(1,), last=(u,), hr=(u + 1,))
+        return dict(ref=ref, h=h, spans=((0, cut), (cut, u - cut)), **where)
+
+    bufs = []
+    cut = (y1.shape[1] - 2) * 5 // 8
+    for ref in (y1, z1, y2, z2, y3):
+        bufs.append(buf(ref, cut))
+        cut = (cut - 1) // 2 if ref is y2 else cut - 1
 
     for b in bufs:
         ref, h = b['ref'], b['h']
@@ -133,11 +136,12 @@
         for k in range(last + 1):
             zero(xt.at[k, xu + 1, 0])
 
-    def row_copy(i, s):
+    def row_copy(i, s, part):
         b = bufs[i]
+        c, w = b['spans'][part]
         ref, h = b['ref'], b['h']
         src, dst, dr = (1, h + 1, -1) if s == 0 else (h, 0, 1)
-        return pltpu.make_async_remote_copy(ref.at[src, b['real']], ref.at[dst, b['real']], row_send.at[i, s], row_recv.at[i, s],
+        return pltpu.make_async_remote_copy(ref.at[src, pl.ds(1 + c, w)], ref.at[dst, pl.ds(1 + c, w)], row_send.at[i, s, part], row_recv.at[i, s, part],
                                             device_id=dev(dr, 0), device_id_type=pl.DeviceIdType.MESH)
 
     def corner_copy(i, s):
@@ -170,13 +174,13 @@
     corners = [(x[0], s) for s, x in enumerate(near[4:])]
     from_corners = [(x[0], s) for s, x in enumerate(near[:3:-1])]
 
-    def send_rows(i):
-        each(ends, lambda s: row_copy(i, s).start())
-        each(corners, lambda s: corner_copy(i, s).start())
-
-    def wait_rows(i):
-        each(from_ends, lambda s: row_copy(i, s).wait_recv())
-        each(from_corners, lambda s: corner_copy(i, s).wait_recv())
+    def send_rows(i, part):
+        each(ends, lambda s: row_copy(i, s, part).start())
+        each(corners[part::2], lambda s: corner_copy(i, s).start())
+
+    def wait_rows(i, part):
+        each(from_ends, lambda s: row_copy(i, s, part).wait_recv())
+        each(from_corners[1 - part::2], lambda s: corner_copy(i, s).wait_recv())
 
     def xcol_copy(k, s):
         src, dst, dc = ((1, 0), (xu + 1, 0), -1) if s == 0 else ((xu, 3), (0, 3), 1)
@@ -274,9 +278,18 @@
     def finish(acc, bias):
         return jnp.maximum(acc + bias, 0.0).astype(BF)
 
-    def put_pairs(ref, i, v):
+    def put_pairs(ref, i, c, w, v):
         for j in range(2):
-            ref[i + 1, pl.ds(1, pairs), j] = v[:, j * LANES:(j + 1) * LANES].reshape(pairs, nimg, LANES)
+            ref[i + 1, pl.ds(1 + c, w), j] = v[:, j * LANES:(j + 1) * LANES].reshape(w, nimg, LANES)
+
+    def strips_dot(group, taps, dot, put):
+        lhs = [jnp.concatenate([tap(*strip) for strip in group], axis=0) for tap in taps]
+        v = dot(jnp.concatenate(lhs, axis=-1))
+        at = 0
+        for i, c, w in group:
+            m = v.shape[0] * w // sum(strip[2] for strip in group)
+            put(i, c, w, v[at:at + m])
+            at += m
 
     def rows_of(ref, idx, w):
         v = ref[idx]
@@ -289,45 +302,48 @@
         up_now = (t + n - p) // n
         return (1 - up_now) * (n - 1 - t) + up_now * (t - p)
 
-    def wait_conv(i, t, a, h, p):
+    def conv_waits(i, p):
+        h = bufs[i]['h']
         n = h // 2
         seen = n - 1 - p if p else n
 
-        if p:
-            @pl.when(t == 0)
+        def waits(t, a):
+            if p:
+                @pl.when(t == 0)
+                def _():
+                    wait_pair(i, n - 1, h)
+
+                @pl.when(t < p)
+                def _():
+                    wait_pair(i, a - 1, h)
+
+            @pl.when((t > p) & (a + 1 < seen))
             def _():
-                wait_pair(i, n - 1, h)
-
-            @pl.when(t < p)
+                wait_pair(i, a + 1, h)
+
+        def edge_waits():
+            wait_pair(i, 0, h)
+            wait_pair(i, 1, h)
+        return waits, edge_waits, lambda part: wait_rows(i, part)
+
+    def down_waits(i):
+        h = bufs[i]['h']
+
+        def waits(t, a):
+            wait_pair(i, 2 * a + 1, h)
+
+            @pl.when(a < h // 4 - 1)
             def _():
-                wait_pair(i, a - 1, h)
-
-        @pl.when(t == p)
-        def _():
-            wait_pair(i, 0, h)
-            wait_rows(i)
-
-        @pl.when(jnp.logical_and(t >= p, a + 1 < seen))
-        def _():
-            wait_pair(i, a + 1, h)
-
-    def wait_down(i, a, h):
-        @pl.when(a == 0)
-        def _():
-            wait_pair(i, 0, 2 * h)
-            wait_rows(i)
-        wait_pair(i, 2 * a + 1, 2 * h)
-
-        @pl.when(a < h // 2 - 1)
-        def _():
-            wait_pair(i, 2 * a + 2, 2 * h)
-
-    def send(i, t, a, h, e):
-        each(sides, lambda s: [col_copy(i, r, s).start() for r in (a, h - 1 - a)])
-
-        @pl.when(t == e)
-        def _():
-            send_rows(i)
+                wait_pair(i, 2 * a + 2, h)
+
+        def edge_waits():
+            for r in range(3):
+                wait_pair(i, r, h)
+        return waits, edge_waits, lambda part: wait_rows(i, part)
+
+    def run(made):
+        body, count = made
+        lax.fori_loop(0, count, body, 0)
 
     pairs = y1.shape[1] - 2
     bias1 = jnp.concatenate([vb1[...], vb1[...]], axis=-1)
@@ -335,9 +351,7 @@
 
     e1 = 4
 
-    def down1(t, carry):
-        a = step_of(t, h1 // 2, e1)
-
+    def down1_waits(t, a):
         @pl.when(t == 0)
         def _():
             wait_xcols(mid)
@@ -346,23 +360,51 @@
         def _():
             wait_xcols(a, last - a)
 
-        @pl.when(t == e1)
-        def _():
-            wait_xcols(0, last)
-
-        @pl.when(jnp.logical_and(t >= e1, a + 1 < h1 // 2 - e1))
+        @pl.when((t > e1) & (a + 1 < h1 // 2 - e1))
         def _():
             wait_xcols(a + 1, last - 1 - a)
-        for i in (a, h1 - 1 - a):
-            parts = []
-            for dk in range(2):
-                for p in range(3, 9):
-                    parts.append(rows_of(xt, (i + dk, pl.ds(p // 4, pairs), p % 4), pairs))
-            acc = jnp.dot(jnp.concatenate(parts, axis=-1), wp1[...].reshape(6 * TILE, TILE), preferred_element_type=F32)
-            v = finish(acc, bias1)
-            put_pairs(y1, i, v)
-        send(0, t, a, h1, e1)
-        return carry
+
+    def layer(i, p, waits, edge_waits, part_waits, taps, dot, put, join=False):
+        b = bufs[i]
+        h = b['h']
+        width = sum(b['spans'][1])
+
+        def body(t, carry):
+            a = step_of(t, h // 2, p)
+
+            @pl.when(t != p)
+            def _():
+                waits(t, a)
+                group = [(a, 0, width), (h - 1 - a, 0, width)]
+                for g in [group] if join else [group[:1], group[1:]]:
+                    strips_dot(g, taps, dot, put)
+                each(sides, lambda s: [col_copy(i, r, s).start() for r in (a, h - 1 - a)])
+
+            @pl.when(t == p)
+            def _():
+                edge_waits()
+                for part in range(2):
+                    part_waits(part)
+                    strips_dot([(r, *b['spans'][part]) for r in (0, h - 1)], taps, dot, put)
+                    send_rows(i, part)
+                    each(sides[part:part + 1], lambda s: [col_copy(i, r, s).start() for r in (0, h - 1)])
+            return carry
+        return body, h // 2
+
+    def tap_of(ref, stride, p, s):
+        if len(ref.shape) > 4:
+            return lambda i, c, w: rows_of(ref, (stride * i + p, pl.ds(c + (s + 1) // 2, w), (s + 1) % 2), w)
+        return lambda i, c, w: rows_of(ref, (i + p, pl.ds(c + s, w)), w)
+
+    def relu_dot(weight, bias):
+        return lambda lhs: finish(jnp.dot(lhs, weight(), preferred_element_type=F32), bias)
+
+    def image_tap(dk, p):
+        return lambda i, c, w: rows_of(xt, (i + dk, pl.ds(c + p // 4, w), p % 4), w)
+
+    down1, _ = layer(0, e1, down1_waits, lambda: wait_xcols(0, last, 1, last - 1), lambda part: None,
+                     [image_tap(dk, p) for dk in range(2) for p in range(3, 9)],
+                     relu_dot(lambda: wp1[...].reshape(6 * TILE, TILE), bias1), functools.partial(put_pairs, y1))
 
     def phase(ph, carry):
         lax.fori_loop(inner * ph, inner + ph, take_three, 0)
@@ -379,21 +421,8 @@
 
     bias2 = jnp.concatenate([vb2[...], vb2[...]], axis=-1)
 
-    def conv1(t, carry):
-        a = step_of(t, h1 // 2, 2)
-        wait_conv(0, t, a, h1, 2)
-        for i in (a, h1 - 1 - a):
-            parts = []
-            for p in range(3):
-                for s in range(1, 5):
-                    parts.append(rows_of(y1, (i + p, pl.ds(s // 2, pairs), s % 2), pairs))
-            acc = jnp.dot(jnp.concatenate(parts, axis=-1), wp2[...].reshape(6 * TILE, TILE), preferred_element_type=F32)
-            v = finish(acc, bias2)
-            put_pairs(z1, i, v)
-        send(1, t, a, h1, 2)
-        return carry
-
-    lax.fori_loop(0, h1 // 2, conv1, 0)
+    run(layer(1, 2, *conv_waits(0, 2), [tap_of(y1, 1, p, s) for p in range(3) for s in range(4)],
+              relu_dot(lambda: wp2[...].reshape(6 * TILE, TILE), bias2), functools.partial(put_pairs, z1)))
 
     ch3 = out.shape[-1]
     h2 = y2.shape[0] - 2
@@ -401,20 +430,11 @@
     for i in (2, 8):
         wcopies[i].wait()
 
-    def down2(t, carry):
-        a = t
-        wait_down(1, a, h2)
-        for i in (a, h2 - 1 - a):
-            parts = []
-            for p in range(4):
-                for s in range(1, 5):
-                    parts.append(rows_of(z1, (2 * i + p, pl.ds(s // 2, w2), s % 2), w2))
-            acc = jnp.dot(jnp.concatenate(parts, axis=-1), vwd2[...].reshape(16 * LANES, TILE), preferred_element_type=F32)
-            y2[i + 1, pl.ds(1, w2)] = finish(acc, vb3[...]).reshape(w2, nimg, TILE)
-        send(2, t, a, h2, 0)
-        return carry
-
-    lax.fori_loop(0, h2 // 2, down2, 0)
+    def put_flat(ref, i, c, w, v):
+        ref[i + 1, pl.ds(1 + c, w)] = v.reshape(w, nimg, v.shape[-1])
+
+    run(layer(2, 0, *down_waits(1), [tap_of(z1, 2, p, s) for p in range(4) for s in range(4)],
+              relu_dot(lambda: vwd2[...].reshape(16 * LANES, TILE), vb3[...]), functools.partial(put_flat, y2)))
     for i in (3, 9, 5):
         wcopies[i].wait()
 
@@ -424,53 +444,37 @@
 
     loop(9, fill6)
 
-    def conv2(t, carry):
-        a = t
-        wait_conv(2, t, a, h2, 0)
-        for i in (a, h2 - 1 - a):
-            parts = []
-            for p in range(3):
-                for q in range(3):
-                    parts.append(rows_of(y2, (i + p, pl.ds(q, w2)), w2))
-            acc = jnp.dot(jnp.concatenate(parts, axis=-1), vwc2[...].reshape(9 * TILE, TILE), preferred_element_type=F32)
-            v = finish(acc, vb4[...]).reshape(w2 // 2, 2, nimg, TILE)
-            z2[i + 1, pl.ds(1, w2 // 2), 0] = v[:, 0]
-            z2[i + 1, pl.ds(1, w2 // 2), 1] = v[:, 1]
-        send(3, t, a, h2, 0)
-        return carry
-
-    lax.fori_loop(0, h2 // 2, conv2, 0)
+    def put_even_odd(i, c, w, v):
+        v = v.reshape(w, 2, nimg, v.shape[-1])
+        for j in range(2):
+            z2[i + 1, pl.ds(1 + c, w), j] = v[:, j]
+
+    def pair_tap(p, q):
+        return lambda i, c, w: rows_of(y2, (i + p, pl.ds(2 * c + q, 2 * w)), 2 * w)
+
+    run(layer(3, 0, *conv_waits(2, 0), [pair_tap(p, q) for p in range(3) for q in range(3)],
+              relu_dot(lambda: vwc2[...].reshape(9 * TILE, TILE), vb4[...]), put_even_odd))
 
     h3 = y3.shape[0] - 2
     w3 = y3.shape[1] - 2
     for i in (4, 10, 11):
         wcopies[i].wait()
 
-    def down3(t, carry):
-        a = t
-        wait_down(3, a, h3)
-        ii = (a, h3 - 1 - a)
-        parts, wts = [], []
-        for p in range(4):
-            for s in range(1, 5):
-                parts.append(jnp.concatenate([rows_of(z2, (2 * i + p, pl.ds(s // 2, w3), s % 2), w3) for i in ii], axis=0))
-                wts.append(vwd3[p, s - 1])
-        acc = lax.dot_general(jnp.concatenate(parts, axis=-1), jnp.concatenate(wts, axis=-1), BY_LAST, preferred_element_type=F32)
-        v = finish(acc, vb5[...])
-        v = jnp.concatenate([v, jnp.zeros((v.shape[0], y3.shape[-1] - ch3), BF)], axis=-1)
-        for n, i in enumerate(ii):
-            y3[i + 1, pl.ds(1, w3)] = v[n * w3 * nimg:(n + 1) * w3 * nimg].reshape(w3, nimg, y3.shape[-1])
-        send(4, t, a, h3, 0)
-        return carry
-
-    lax.fori_loop(0, h3 // 2, down3, 0)
+    def down3_dot(lhs):
+        wts = jnp.concatenate([vwd3[p, q] for p in range(4) for q in range(4)], axis=-1)
+        v = finish(lax.dot_general(lhs, wts, BY_LAST, preferred_element_type=F32), vb5[...])
+        return jnp.concatenate([v, jnp.zeros((v.shape[0], y3.shape[-1] - ch3), BF)], axis=-1)
+
+    run(layer(4, 0, *down_waits(3), [tap_of(z2, 2, p, s) for p in range(4) for s in range(4)],
+              down3_dot, functools.partial(put_flat, y3), join=True))
 
     def conv3(t, carry):
         @pl.when(t == 1)
         def _():
             for r in range(h3 // 2):
                 wait_pair(4, r, h3)
-            wait_rows(4)
+            for part in range(2):
+                wait_rows(4, part)
         top, bottom, lo, hi = 1 - t, h3 - 2 + t, 1 - t, w3 - 2 + t
         strips = [(i, 1, w3 - 2) for i in (top, bottom)] + [(i, c, 1) for i in (top, bottom, *range(1, h3 - 1)) for c in (lo, hi)]
         parts = []
@@ -495,7 +499,8 @@
 
     each(sides, lambda s: drain_cols(xt, pl.ds(0, last + 1), (1, 0), xc_send.at[s]))
     for i, b in enumerate(bufs):
-        each(ends, lambda s: row_copy(i, s).wait_send())
+        for part in range(2):
+            each(ends, lambda s: row_copy(i, s, part).wait_send())
         each(corners, lambda s: corner_copy(i, s).wait_send())
         each(sides, lambda s: drain_cols(b['ref'], pl.ds(1, b['h']), b['first'], col_send.at[i, s]))
 
@@ -529,7 +534,7 @@
             pltpu.VMEM((12, c1, TILE), BF),
             pltpu.VMEM((9, c3p, c3), BF),
         ] + [pltpu.VMEM((1, k), F32) for k in (c1, c1, c2, c2, c3, c3)] + [
-            dma(d) for d in ((kk,), (12,), (2,), (2,), (2,), (kk, 2), (5, 2), (5, 2), (5, 4), (5, 4), (5, 2), (5, hh, 2))
+            dma(d) for d in ((kk,), (12,), (2,), (2,), (2,), (kk, 2), (5, 2, 2), (5, 2, 2), (5, 4), (5, 4), (5, 2), (5, hh, 2))
         ]
         feats = pl.pallas_call(
             functools.partial(_encoder_kernel, dims),

time: 60.2 us -> 62.8 us (1.043)
  Pallas kernels: 57.8 us -> 60.5 us
    pallas_call x1, Pallas kernels: 57.8 us -> 60.5 us  [local_encoder(): pl.pallas_call(functools.partial(_encoder_kernel, dims), out_shape=jax.Sh...]
where the time goes in v6:
time: 62.8 us; the launch traced here: 62.7 us
  Pallas kernels  60.5 us (96%)
  local copies, waits for them, and re-layouts  2.2 us (4%)
    pallas_call x1, Pallas kernels, local_encoder(): pl.pallas_call(functools.partial(_encoder_kernel, dims), out_shape=jax.Sh...  60.5 us
    transpose x1, local copies, waits for them, and re-layouts, local_encoder(): return jnp.transpose(feats, (2, 0, 1, 3))  2.2 us

profile of v6, /device:TPU:97, one launch (start us, length us, event | category | flops | bytes accessed | tf_op | source)
XLA Modules:
  0.0 62.7 jit_solution(9738561290471486353)
XLA Ops:
  0.0 60.5 %shard_map.127 = bf16[4,16,16,320]{3,2,1,0:T(8,128)(2,1)} custom-call(bf16[16,32,64,128]{3,2,1,0:T(8,128)(2,1)} %bitcast.3, bf16[4,4,64,128]{3,2,1,0:T(8,128)(2,1)} %wd1.1, f32[128]{0:T(128)} %bd1.1, bf16[3,3,128,128]{3,2,1,0:T(8,128)(2,1)} %wc1.1, f32[128]{0:T(128)} %bc1.1, bf16[4,4,128,256]{3,2,1,0:T(8,128)(2,1)} %wd2.1, f32[256]{0:T(256)} %bd2.1, ...), custom_call_target="tpu_custom_call" | custom-call | tf_op jit(solution)/shard_map/pallas_call | solution.py:539
  60.5 2.2 %copy.14 = bf16[16,4,16,320]{3,2,1,0:T(8,128)(2,1)} copy(bf16[16,4,16,320]{3,0,2,1:T(8,128)(2,1)} %bitcast.4) | data formatting | bytes 1310720 | tf_op jit(solution)/shard_map/transpose | solution.py:547

commit v7 on v5

--- a/solution.py
+++ b/solution.py
@@ -44,17 +44,24 @@
     mid = last // 2
     first_copy = pltpu.make_async_copy(img.at[:, pl.ds(0, 1)], raw.at[0, :, pl.ds(1, 1)], raw_sem.at[0])
     last_copy = pltpu.make_async_copy(img.at[:, pl.ds(2 * last - 1, 1)], raw.at[last, :, pl.ds(0, 1)], raw_sem.at[last])
-    order = []
-    for t in range(last - 1):
+    def loop(count, act):
+        def body(i, carry):
+            act(i)
+            return carry
+        lax.fori_loop(0, count, body, 0)
+
+    def middle_out(t):
         h = (t + 1) // 2
-        order.append(mid - h if t % 2 else mid + h)
+        return mid + h * (1 - 2 * (t % 2))
+
     weights = [(wd1, vwd1), (wc1, vwc1), (wd2, vwd2), (wc2, vwc2), (wd3, vwd3), (wc3, vwc3),
                *((x, v.at[0]) for x, v in zip((bd1, bc1, bd2, bc2, bd3, bc3), (vb1, vb2, vb3, vb4, vb5, vb6)))]
     wcopies = [pltpu.make_async_copy(s, d, w_sem.at[i]) for i, (s, d) in enumerate(weights)]
     for i in (0, 6, 1, 7):
         wcopies[i].start()
-    for k in order[:6]:
-        raw_copy(k).start()
+    loop(last - 1, lambda t: raw_copy(middle_out(t)).start())
+    first_copy.start()
+    last_copy.start()
 
     barrier = pltpu.get_barrier_semaphore()
     for there, dr, dc in near:
@@ -192,12 +199,6 @@
     for i in (0, 1, 6, 7):
         wcopies[i].wait()
 
-    def loop(count, act):
-        def body(i, carry):
-            act(i)
-            return carry
-        lax.fori_loop(0, count, body, 0)
-
     def zero_block(ref):
         def act(i):
             zero(ref.at[i])
@@ -230,25 +231,11 @@
         for c in range(4 * xu):
             xt[k, 1 + c // 4, c % 4] = st[pl.ds(c, nimg, stride=PITCH), :].astype(BF)
 
-    def middle_out(t):
-        h = (t + 1) // 2
-        return mid + h * (1 - 2 * (t % 2))
-
     inner = (last - 1) // 3
 
     def take_three(it, carry):
         edge = it // inner
         ks = [edge * (last * min(d, 1)) + (1 - edge) * middle_out(3 * it + d) for d in range(3)]
-
-        @pl.when(it < inner - 2)
-        def _():
-            for d in range(3):
-                raw_copy(middle_out(3 * it + 6 + d)).start()
-
-        @pl.when(it == inner - 2)
-        def _():
-            first_copy.start()
-            last_copy.start()
 
         @pl.when(it < inner)
         def _():
@@ -323,11 +310,10 @@
             wait_pair(i, 2 * a + 2, 2 * h)
 
     def send(i, t, a, h, e):
+        @pl.when(t == e)
+        def _():
+            send_rows(i)
         each(sides, lambda s: [col_copy(i, r, s).start() for r in (a, h - 1 - a)])
-
-        @pl.when(t == e)
-        def _():
-            send_rows(i)
 
     pairs = y1.shape[1] - 2
     bias1 = jnp.concatenate([vb1[...], vb1[...]], axis=-1)
@@ -537,8 +523,8 @@
             in_specs=[hbm] * 13,
             out_specs=pl.BlockSpec(memory_space=pltpu.VMEM),
             scratch_shapes=scratch,
-            compiler_params=pltpu.CompilerParams(collective_id=0, has_side_effects=True, vmem_limit_bytes=62 * 1024 * 1024),
-        )(img, w_down1, b_down1, w_conv1, b_conv1, w_down2, b_down2, w_conv2, b_conv2, wd3, b_down3, w_conv3, b_conv3)
+            compiler_params=pltpu.CompilerParams(collective_id=0, has_side_effects=True, vmem_limit_bytes=53 * 1024 * 1024),
+        )(*[pltpu.with_memory_space_constraint(x, pltpu.HBM) for x in (img, w_down1, b_down1, w_conv1, b_conv1, w_down2, b_down2, w_conv2, b_conv2, wd3, b_down3, w_conv3, b_conv3)])
         return jnp.transpose(feats, (2, 0, 1, 3))
 
     tile_spec = P('batch', 'row', 'col', None)

time: 60.2 us -> 57.7 us (0.958)
  Pallas kernels: 57.8 us -> 56.5 us
  local copies, waits for them, and re-layouts: 2.2 us -> 1.06 us
    pallas_call x1, Pallas kernels: 57.8 us -> 56.5 us  [local_encoder(): pl.pallas_call(functools.partial(_encoder_kernel, dims), out_shape=jax.Sh...]
    transpose x1, local copies, waits for them, and re-layouts: 2.2 us -> 1.06 us  [local_encoder(): return jnp.transpose(feats, (2, 0, 1, 3))]
where the time goes in v7:
time: 57.7 us; the launch traced here: 57.6 us
  Pallas kernels  56.5 us (98%)
  local copies, waits for them, and re-layouts  1.06 us (2%)
    pallas_call x1, Pallas kernels, local_encoder(): pl.pallas_call(functools.partial(_encoder_kernel, dims), out_shape=jax.Sh...  56.5 us

profile of v7, /device:TPU:97, one launch (start us, length us, event | category | flops | bytes accessed | tf_op | source)
XLA Modules:
  0.0 57.6 jit_solution(15754224127436058971)
XLA Ops:
  0.0 56.5 %shard_map.127 = bf16[4,16,16,320]{3,2,1,0:T(8,128)(2,1)S(1)} custom-call(bf16[16,32,64,128]{3,2,1,0:T(8,128)(2,1)} %bitcast.4, bf16[4,4,64,128]{3,2,1,0:T(8,128)(2,1)} %wd1.1, f32[128]{0:T(128)} %bd1.1, bf16[3,3,128,128]{3,2,1,0:T(8,128)(2,1)} %wc1.1, f32[128]{0:T(128)} %bc1.1, bf16[4,4,128,256]{3,2,1,0:T(8,128)(2,1)} %wd2.1, f32[256]{0:T(256)} %bd2.1, ...), custom_call_target="tpu_custom_call" | custom-call | tf_op jit(solution)/shard_map/pallas_call | solution.py:520
  56.6 1.1 %copy.14 = bf16[16,4,16,320]{3,2,1,0:T(8,128)(2,1)} copy(bf16[16,4,16,320]{3,0,2,1:T(8,128)(2,1)S(1)} %bitcast.3) | data formatting | bytes 1310720 | tf_op jit(solution)/shard_map/transpose | solution.py:528

commit v8 on v7

--- a/solution.py
+++ b/solution.py
@@ -319,7 +319,7 @@
     bias1 = jnp.concatenate([vb1[...], vb1[...]], axis=-1)
     h1 = y1.shape[0] - 2
 
-    e1 = 4
+    e1 = 3
 
     def down1(t, carry):
         a = step_of(t, h1 // 2, e1)
@@ -366,8 +366,8 @@
     bias2 = jnp.concatenate([vb2[...], vb2[...]], axis=-1)
 
     def conv1(t, carry):
-        a = step_of(t, h1 // 2, 2)
-        wait_conv(0, t, a, h1, 2)
+        a = step_of(t, h1 // 2, 1)
+        wait_conv(0, t, a, h1, 1)
         for i in (a, h1 - 1 - a):
             parts = []
             for p in range(3):
@@ -376,7 +376,7 @@
             acc = jnp.dot(jnp.concatenate(parts, axis=-1), wp2[...].reshape(6 * TILE, TILE), preferred_element_type=F32)
             v = finish(acc, bias2)
             put_pairs(z1, i, v)
-        send(1, t, a, h1, 2)
+        send(1, t, a, h1, 1)
         return carry
 
     lax.fori_loop(0, h1 // 2, conv1, 0)

time: 57.7 us -> 57.5 us (level)
  no operation moved by 1% of the time
where the time goes in v8:
time: 57.5 us
  Pallas kernels  56.4 us (98%)
  local copies, waits for them, and re-layouts  1.06 us (2%)
    pallas_call x1, Pallas kernels, local_encoder(): pl.pallas_call(functools.partial(_encoder_kernel, dims), out_shape=jax.Sh...  56.4 us

profile of v8, /device:TPU:97, one launch (start us, length us, event | category | flops | bytes accessed | tf_op | source)
XLA Modules:
  0.0 57.5 jit_solution(6867492046535099632)
XLA Ops:
  0.0 56.4 %shard_map.127 = bf16[4,16,16,320]{3,2,1,0:T(8,128)(2,1)S(1)} custom-call(bf16[16,32,64,128]{3,2,1,0:T(8,128)(2,1)} %bitcast.4, bf16[4,4,64,128]{3,2,1,0:T(8,128)(2,1)} %wd1.1, f32[128]{0:T(128)} %bd1.1, bf16[3,3,128,128]{3,2,1,0:T(8,128)(2,1)} %wc1.1, f32[128]{0:T(128)} %bc1.1, bf16[4,4,128,256]{3,2,1,0:T(8,128)(2,1)} %wd2.1, f32[256]{0:T(256)} %bd2.1, ...), custom_call_target="tpu_custom_call" | custom-call | tf_op jit(solution)/shard_map/pallas_call | solution.py:520
  56.4 1.1 %copy.14 = bf16[16,4,16,320]{3,2,1,0:T(8,128)(2,1)} copy(bf16[16,4,16,320]{3,0,2,1:T(8,128)(2,1)S(1)} %bitcast.3) | data formatting | bytes 1310720 | tf_op jit(solution)/shard_map/transpose | solution.py:528
